TPU v7x, 32 devices: a whole 2x2x4 slice. The times are simulated.
32 devices in a mesh: ctx: 8 (over z, x), head: 4 (over y, core).
Axes of the slice: x: 2, y: 2, z: 4, core: 2. Of those that a mesh axis runs over, the one named last changes fastest.
Arguments:
- queries: bfloat16 [4096, 4096], P('ctx', 'head'), may hold values from -6 to 6
- keys: bfloat16 [2, 4096, 4096], P(None, 'ctx', 'head'), may hold values from -6 to 6
- values: bfloat16 [2, 4096, 4096], P(None, 'ctx', 'head'), may hold values from -6 to 6
- betas: float32 [32, 2, 4096], P('head', None, 'ctx'), may hold values from 1.9 to 2
- gate: bfloat16 [4096, 4096], P('ctx', 'head'), may hold values from -6 to 6
- out_weight: bfloat16 [4096, 4096], P('head'), may hold values from -0.125 to 0.125
Outputs:
- mixed: bfloat16 [4096, 4096], P('ctx', 'head')
All inputs are finite; a program needn't handle non-finite values.
Results may differ from a plain program's by a relative error of at most 0.02.
Values may be sent and summed in bfloat16 or wider, within the bound.
A program may use at most 128 MiB of HBM per device.

v0:
```python
import functools

import jax
import jax.numpy as jnp
from jax import lax
from jax.experimental import pallas as pl
from jax.experimental.pallas import tpu as pltpu
from jax.sharding import PartitionSpec as P

HEAD_DIM = 128
SPAN = 64
BASE = 16
F32 = jnp.float32
BF16 = jnp.bfloat16
VMEM_LIMIT = 60 * 1024 * 1024
MESH = pl.DeviceIdType.MESH
PIECES = 4


def iota(shape, dim):
    return lax.broadcasted_iota(jnp.int32, shape, dim)


def split(a):
    high = a.astype(BF16)
    return high, (a - high.astype(F32)).astype(BF16)


def dot(a, b):
    return jnp.dot(a, b, preferred_element_type=F32)


def dot3(a, b):
    ah, al = split(a)
    bh, bl = split(b)
    return dot(jnp.concatenate([ah, al, ah], axis=1), jnp.concatenate([bh, bh, bl], axis=0))


def inverse(lowers, order):
    lane = iota((BASE, order), 1)
    compact = []
    for low in lowers:
        total = jnp.zeros((BASE, order), F32)
        for blk in range(order // BASE):
            total = jnp.where(lane // BASE == blk, low[blk * BASE : (blk + 1) * BASE, :], total)
        compact.append(total)
    inv = [(iota((BASE, order), 0) == lane % BASE).astype(F32) for _ in lowers]
    for j in range(BASE - 1):
        pick = (lane // BASE) * BASE + j
        for n, low in enumerate(compact):
            column = jnp.take_along_axis(low, pick, axis=1, mode="promise_in_bounds")
            inv[n] = inv[n] - column * inv[n][j : j + 1, :]
    row = iota((order, order), 0)
    col = iota((order, order), 1)
    width = BASE
    while width < order:
        corner = (row // (2 * width) == col // (2 * width)) & (row // width != col // width)
        diagonal = row // width == col // width
        second = (iota((width, order), 1) // width) % 2 == 1
        half = [dot3(jnp.where(second, t, 0.0), jnp.where(corner, low, 0.0)) for t, low in zip(inv, lowers)]
        full = [
            jnp.where(diagonal, jnp.concatenate([t] * (order // width), axis=0), 0.0) for t in inv
        ]
        fill = [dot3(y, e) for y, e in zip(half, full)]
        inv = [
            jnp.concatenate([jnp.where(second, 0.0, t), jnp.where(second, t, 0.0) - r], axis=0)
            for t, r in zip(inv, fill)
        ]
        width *= 2
    return inv


def mix_kernel(q_ref, k_ref, v_ref, b_ref, o_ref, m_ref, x_out, x_ref):
    heads = q_ref.shape[1] // HEAD_DIM
    span = q_ref.shape[0]
    order = 2 * span
    step = pl.program_id(0)

    @pl.when(step == 0)
    def _():
        start = (iota((HEAD_DIM, 2 * HEAD_DIM), 0) == iota((HEAD_DIM, 2 * HEAD_DIM), 1)).astype(F32)
        for h in range(heads):
            x_ref[h] = start

    row = iota((order, order), 0)
    col = iota((order, order), 1)
    strict = col < row
    weave = (row == 2 * (col % span) + col // span).astype(BF16)
    causal = iota((span, order), 1) <= 2 * iota((span, order), 0) + 1
    data = []
    lowers = []
    for h in range(heads):
        cols = slice(h * HEAD_DIM, (h + 1) * HEAD_DIM)
        query = q_ref[:, cols]
        pair = jnp.concatenate(
            [
                jnp.concatenate([k_ref[0, :, cols], v_ref[0, :, cols]], axis=1),
                jnp.concatenate([k_ref[1, :, cols], v_ref[1, :, cols]], axis=1),
            ],
            axis=0,
        )
        woven = dot(weave, pair)
        key = woven[:, :HEAD_DIM]
        value = woven[:, HEAD_DIM:]
        key_b = key.astype(BF16)
        norm = lax.rsqrt(jnp.sum(key * key, axis=1, keepdims=True) + 1e-06)
        beta = b_ref[:, h : h + 1]
        both = jnp.concatenate([key_b, query], axis=0)
        gram = lax.dot_general(both, key_b, (((1,), (1,)), ((), ())), preferred_element_type=F32)
        weight = beta * norm * norm
        lowers.append(jnp.where(strict, weight * gram[:order], 0.0))
        scores = jnp.where(causal, gram[order:], 0.0).astype(BF16)
        qf = query.astype(F32)
        q_norm = lax.rsqrt(jnp.sum(qf * qf, axis=1, keepdims=True) + 1e-06)
        readers = jnp.concatenate([key.T.astype(BF16), scores], axis=0)
        data.append((both, readers, beta * norm * value, weight, q_norm))
    solved = inverse(lowers, order)
    seen = []
    for h in range(heads):
        both = data[h][0]
        high, low = split(x_ref[h])
        seen.append(
            dot(jnp.concatenate([both, both], axis=1), jnp.concatenate([high, low], axis=0))
        )
    writes = []
    for h in range(heads):
        _, _, scaled, weight, _ = data[h]
        gap = -weight * seen[h][:order]
        gap = jnp.concatenate([gap[:, :HEAD_DIM], gap[:, HEAD_DIM:] + scaled], axis=1)
        writes.append(dot3(solved[h], gap))
    for h in range(heads):
        cols = slice(h * HEAD_DIM, (h + 1) * HEAD_DIM)
        readers, q_norm = data[h][1], data[h][4]
        high, low = split(writes[h])
        change = dot(
            jnp.concatenate([readers, readers], axis=1), jnp.concatenate([high, low], axis=0)
        )
        x_ref[h] = x_ref[h] + change[:HEAD_DIM]
        out = q_norm * (seen[h][order:] + change[HEAD_DIM:])
        m_ref[:, cols] = out[:, :HEAD_DIM].astype(BF16)
        o_ref[:, cols] = out[:, HEAD_DIM:]

    @pl.when(step == pl.num_programs(0) - 1)
    def _():
        for h in range(heads):
            x_out[h] = x_ref[h].astype(BF16)


def mix(queries, keys, values, beta_cols):
    tokens, width = queries.shape
    heads = width // HEAD_DIM
    return pl.pallas_call(
        mix_kernel,
        grid=(tokens // SPAN,),
        in_specs=[
            pl.BlockSpec((SPAN, width), lambda c: (c, 0)),
            pl.BlockSpec((2, SPAN, width), lambda c: (0, c, 0)),
            pl.BlockSpec((2, SPAN, width), lambda c: (0, c, 0)),
            pl.BlockSpec((2 * SPAN, heads), lambda c: (c, 0)),
        ],
        out_specs=[
            pl.BlockSpec((SPAN, width), lambda c: (c, 0)),
            pl.BlockSpec((SPAN, width), lambda c: (c, 0)),
            pl.BlockSpec((heads, HEAD_DIM, 2 * HEAD_DIM), lambda c: (0, 0, 0)),
        ],
        out_shape=[
            jax.ShapeDtypeStruct((tokens, width), F32),
            jax.ShapeDtypeStruct((tokens, width), BF16),
            jax.ShapeDtypeStruct((heads, HEAD_DIM, 2 * HEAD_DIM), BF16),
        ],
        scratch_shapes=[pltpu.VMEM((heads, HEAD_DIM, 2 * HEAD_DIM), F32)],
        compiler_params=pltpu.CompilerParams(
            dimension_semantics=("arbitrary",), vmem_limit_bytes=VMEM_LIMIT
        ),
    )(queries, keys, values, beta_cols)


def chain_kernel(peers, x_ref, s_ref):
    heads = x_ref.shape[0] // peers
    for h in range(heads):
        state = jnp.zeros((HEAD_DIM, HEAD_DIM), F32)
        for k in range(peers):
            s_ref[k * heads + h] = state.astype(BF16)
            if k < peers - 1:
                maps = x_ref[k * heads + h]
                turn = maps[:, :HEAD_DIM]
                high, low = split(state)
                state = maps[:, HEAD_DIM:].astype(F32) + dot(
                    jnp.concatenate([turn, turn], axis=1), jnp.concatenate([high, low], axis=0)
                )


def exchange(axis, peers, maps_ref, own_ref, held, states, out_send, out_recv, back_send, back_recv):
    me = lax.axis_index(axis)
    heads = maps_ref.shape[0] // peers

    def outward(away):
        peer = lax.rem(me + away, peers)
        return pltpu.make_async_remote_copy(
            src_ref=maps_ref.at[pl.ds(peer * heads, heads)],
            dst_ref=held.at[pl.ds(me * heads, heads)],
            send_sem=out_send.at[away],
            recv_sem=out_recv.at[away],
            device_id={axis: peer},
            device_id_type=MESH,
        )

    def homeward(away):
        peer = lax.rem(me + away, peers)
        return pltpu.make_async_remote_copy(
            src_ref=states.at[pl.ds(peer * heads, heads)],
            dst_ref=own_ref.at[pl.ds(me * heads, heads)],
            send_sem=back_send.at[away],
            recv_sem=back_recv.at[away],
            device_id={axis: peer},
            device_id_type=MESH,
        )

    for away in range(1, peers):
        outward(away).start()
    for h in range(heads):
        held[me * heads + h] = maps_ref[me * heads + h]
    for away in range(1, peers):
        outward(away).wait()
    chain_kernel(peers, held, states)
    for away in range(1, peers):
        homeward(away).start()
    for h in range(heads):
        own_ref[me * heads + h] = states[me * heads + h]
    for away in range(1, peers):
        homeward(away).wait()


def start_state(maps, axis):
    peers, index = lax.axis_size(axis), lax.axis_index(axis)
    heads = maps.shape[0]
    held = lax.all_gather(maps, axis, axis=0, tiled=True)
    states = pl.pallas_call(
        functools.partial(chain_kernel, peers),
        out_shape=jax.ShapeDtypeStruct((held.shape[0], HEAD_DIM, HEAD_DIM), BF16),
        compiler_params=pltpu.CompilerParams(vmem_limit_bytes=VMEM_LIMIT),
    )(held)
    return lax.dynamic_slice_in_dim(states, index * heads, heads, 0)


def finish_kernel(
    seq_axis, seq_peers, axis, maps_ref, o_hbm, m_hbm, g_hbm, w_ref, y_ref,
    held, states, s_ref, o_ref, m_ref, g_ref,
    mixed, weight, total, far_out, far_in, near_out, near_in, cross_out, cross_in,
    out_send, out_recv, back_send, back_recv, fetch_sem,
    load_sem, far_send, far_recv, near_send, near_recv, cross_send, cross_recv,
):
    me = lax.axis_index(axis)
    chip, core = me // 2, me % 2
    sibling = 2 * chip + 1 - core
    across = 2 * (1 - chip) + core
    beyond = 2 * (1 - chip) + 1 - core
    width = y_ref.shape[1]
    rows = y_ref.shape[0] // PIECES

    fetches = [
        pltpu.make_async_copy(source, target, fetch_sem.at[n])
        for n, (source, target) in enumerate(((o_hbm, o_ref), (m_hbm, m_ref), (g_hbm, g_ref)))
    ]
    loads = []
    for n, owner in enumerate((beyond, across, sibling, me)):
        loads.append(
            pltpu.make_async_copy(
                w_ref.at[:, pl.ds(pl.multiple_of(owner * width, width), width)],
                weight.at[n],
                load_sem.at[n],
            )
        )

    barrier = pltpu.get_barrier_semaphore()
    for other in (sibling, across):
        pl.semaphore_signal(barrier, inc=1, device_id={axis: other}, device_id_type=MESH)
    for away in range(1, seq_peers):
        pl.semaphore_signal(
            barrier,
            inc=1,
            device_id={seq_axis: lax.rem(lax.axis_index(seq_axis) + away, seq_peers)},
            device_id_type=MESH,
        )
    for copy in fetches + loads:
        copy.start()
    pl.semaphore_wait(barrier, seq_peers + 1)
    exchange(
        seq_axis, seq_peers, maps_ref, s_ref, held, states, out_send, out_recv, back_send, back_recv
    )
    for copy in fetches:
        copy.wait()

    def send(source, target, send_sem, recv_sem, t, device):
        return pltpu.make_async_remote_copy(
            src_ref=source.at[t],
            dst_ref=target.at[t],
            send_sem=send_sem.at[t],
            recv_sem=recv_sem.at[t],
            device_id={axis: device},
            device_id_type=MESH,
        )

    def far(t):
        return send(far_out, far_in, far_send, far_recv, t, sibling)

    def near(t):
        return send(near_out, near_in, near_send, near_recv, t, sibling)

    def cross(t):
        return send(cross_out, cross_in, cross_send, cross_recv, t, across)

    def pass_on(t):
        far(t).wait()
        cross_out[t] = (total[t] + far_in[t].astype(F32)).astype(BF16)
        cross(t).start()

    for t in range(PIECES):
        span = slice(t * rows, (t + 1) * rows)
        for h in range(s_ref.shape[0]):
            cols = slice(h * HEAD_DIM, (h + 1) * HEAD_DIM)
            seen = o_ref[span, cols] + dot(m_ref[span, cols], s_ref[h])
            scale = lax.rsqrt(jnp.mean(seen * seen, axis=1, keepdims=True) + 1e-06)
            gate = g_ref[span, cols].astype(F32)
            mixed[t, :, cols] = (seen * scale * (gate / (1.0 + jnp.exp(-gate)))).astype(BF16)
        if t == 0:
            loads[0].wait()
        far_out[t] = dot(mixed[t], weight[0]).astype(BF16)
        far(t).start()
        if t == 0:
            loads[1].wait()
        total[t] = dot(mixed[t], weight[1])
        if t > 0:
            pass_on(t - 1)
    loads[2].wait()
    for t in range(PIECES):
        near_out[t] = dot(mixed[t], weight[2]).astype(BF16)
        near(t).start()
        if t == 0:
            pass_on(PIECES - 1)
    loads[3].wait()
    for t in range(PIECES):
        total[t] = dot(mixed[t], weight[3])
    for t in range(PIECES):
        near(t).wait()
        cross(t).wait()
        y_ref[t * rows : (t + 1) * rows, :] = (
            total[t] + near_in[t].astype(F32) + cross_in[t].astype(F32)
        ).astype(BF16)


def finish(maps, local, reach, gate, out_weight, seq_axis, axis):
    tokens, depth = local.shape
    peers = lax.axis_size(seq_axis)
    width = out_weight.shape[1] // lax.axis_size(axis)
    vmem = pl.BlockSpec(memory_space=pltpu.VMEM)
    hbm = pl.BlockSpec(memory_space=pl.ANY)
    piece = (PIECES, tokens // PIECES, width)
    states = (maps.shape[0], HEAD_DIM, HEAD_DIM)
    return pl.pallas_call(
        functools.partial(finish_kernel, seq_axis, peers, axis),
        in_specs=[vmem, hbm, hbm, hbm, hbm],
        out_specs=vmem,
        out_shape=jax.ShapeDtypeStruct((tokens, width), BF16),
        scratch_shapes=[
            pltpu.VMEM(maps.shape, BF16),
            pltpu.VMEM(states, BF16),
            pltpu.VMEM(states, BF16),
            pltpu.VMEM(local.shape, F32),
            pltpu.VMEM(local.shape, BF16),
            pltpu.VMEM(local.shape, BF16),
            pltpu.VMEM((PIECES, tokens // PIECES, depth), BF16),
            pltpu.VMEM((4, depth, width), BF16),
            pltpu.VMEM(piece, F32),
        ]
        + [pltpu.VMEM(piece, BF16)] * 6
        + [pltpu.SemaphoreType.DMA((peers,))] * 4
        + [pltpu.SemaphoreType.DMA((3,))]
        + [pltpu.SemaphoreType.DMA((4,))]
        + [pltpu.SemaphoreType.DMA((PIECES,))] * 6,
        compiler_params=pltpu.CompilerParams(
            collective_id=0, has_side_effects=True, vmem_limit_bytes=VMEM_LIMIT
        ),
    )(maps, local, reach, gate, out_weight)


def out_kernel(o_ref, m_ref, s_ref, g_ref, w_ref, y_ref, mixed_ref):
    @pl.when(pl.program_id(0) == 0)
    def _():
        for h in range(s_ref.shape[0]):
            cols = slice(h * HEAD_DIM, (h + 1) * HEAD_DIM)
            seen = o_ref[:, cols] + dot(m_ref[:, cols], s_ref[h])
            scale = lax.rsqrt(jnp.mean(seen * seen, axis=1, keepdims=True) + 1e-06)
            gate = g_ref[:, cols].astype(F32)
            mixed_ref[:, cols] = (seen * scale * (gate / (1.0 + jnp.exp(-gate)))).astype(BF16)

    y_ref[...] = dot(mixed_ref[...], w_ref[...]).astype(BF16)


def project(local, reach, states, gate, out_weight):
    tokens, width = local.shape
    total = out_weight.shape[1]
    tile = 512
    whole = pl.BlockSpec((tokens, width), lambda n: (0, 0))
    return pl.pallas_call(
        out_kernel,
        grid=(total // tile,),
        in_specs=[
            whole,
            whole,
            pl.BlockSpec(states.shape, lambda n: (0, 0, 0)),
            whole,
            pl.BlockSpec((width, tile), lambda n: (0, n)),
        ],
        out_specs=pl.BlockSpec((tokens, tile), lambda n: (0, n)),
        out_shape=jax.ShapeDtypeStruct((tokens, total), BF16),
        scratch_shapes=[pltpu.VMEM((tokens, width), BF16)],
        compiler_params=pltpu.CompilerParams(
            dimension_semantics=("arbitrary",), vmem_limit_bytes=VMEM_LIMIT
        ),
    )(local, reach, states, gate, out_weight)


def per_device(queries, keys, values, betas, gate, out_weight):
    heads, _, tokens = betas.shape
    beta_cols = betas.transpose(2, 1, 0).reshape(2 * tokens, heads)
    local, reach, maps = mix(queries, keys, values, beta_cols)
    if lax.axis_size("head") == 4 and heads % lax.axis_size("ctx") == 0:
        return finish(maps, local, reach, gate, out_weight, "ctx", "head")
    states = start_state(maps, "ctx")
    partial_sum = project(local, reach, states, gate, out_weight)
    return lax.psum_scatter(partial_sum, "head", scatter_dimension=1, tiled=True)


def solution(mesh):
    return jax.shard_map(
        per_device,
        mesh=mesh,
        in_specs=(
            P("ctx", "head"),
            P(None, "ctx", "head"),
            P(None, "ctx", "head"),
            P("head", None, "ctx"),
            P("ctx", "head"),
            P("head", None),
        ),
        out_specs=P("ctx", "head"),
        check_vma=False,
    )
```

profile of v0, /device:TPU:24, one launch (start us, length us, event | category | flops | bytes accessed | tf_op | source)
XLA Modules:
  0.0 88.5 jit_solution(13962529142686109719)
XLA Ops:
  0.0 1.8 %copy.7 = f32[512,2,8]{2,1,0:T(2,128)} copy(f32[512,2,8]{0,1,2:T(2,128)} %bitcast.3) | data formatting | bytes 65536 | tf_op jit(solution)/shard_map/transpose | solution.py:426
  1.8 30.9 %shard_map.64 = (f32[512,1024]{1,0:T(8,128)}, bf16[512,1024]{1,0:T(8,128)(2,1)}, bf16[8,128,256]{2,1,0:T(8,128)(2,1)}) custom-call(bf16[512,1024]{1,0:T(8,128)(2,1)} %q_ref.1, bf16[2,512,1024]{2,1,0:T(8,128)(2,1)} %k_ref.1, bf16[2,512,1024]{2,1,0:T(8,128)(2,1)} %v_ref.1, f32[1024,8]{1,0:T(8,128)} %bitcast.2), custom_call_target="tpu_custom_call" | custom-call | tf_op jit(solution)/shard_map/pallas_call | solution.py:152
  32.7 53.5 %shard_map.65 = bf16[512,1024]{1,0:T(8,128)(2,1)} custom-call(bf16[8,128,256]{2,1,0:T(8,128)(2,1)} %get-tuple-element.8.maps_ref, f32[512,1024]{1,0:T(8,128)} %get-tuple-element.9.o_hbm, bf16[512,1024]{1,0:T(8,128)(2,1)} %get-tuple-element.10.m_hbm, bf16[512,1024]{1,0:T(8,128)(2,1)} %g_hbm.1, bf16[1024,4096]{1,0:T(8,128)(2,1)} %w_ref.1), custom_call_target="tpu_custom_call" | custom-call | tf_op jit(solution)/shard_map/pallas_call | solution.py:360
  86.2 2.3 %copy.9 = bf16[512,1024]{1,0:T(8,128)(2,1)} copy(bf16[512,1024]{1,0:T(8,128)(2,1)} %shard_map.65) | data formatting | bytes 2097152
where the time goes:
time: 90 us; the launch traced here: 88.5 us
  Pallas kernels  84.4 us (94%)
  local copies, waits for them, and re-layouts  4.02 us (4%)
    pallas_call x1, Pallas kernels, finish(): pl.pallas_call(functools.partial(finish_kernel, seq_axis, peers, axis), i...  53.5 us
    pallas_call x1, Pallas kernels, mix(): pl.pallas_call(mix_kernel, grid=(tokens // SPAN,), in_specs=[pl.BlockSpec...  30.9 us
    unnamed x1, local copies, waits for them, and re-layouts  2.26 us

commit v1 on v0

--- a/solution.py
+++ b/solution.py
@@ -190,45 +190,532 @@
                 )
 
 
-def exchange(axis, peers, maps_ref, own_ref, held, states, out_send, out_recv, back_send, back_recv):
+def dot_t(a, b):
+    return lax.dot_general(a, b, (((1,), (1,)), ((), ())), preferred_element_type=F32)
+
+
+def pair_dot(a, low, high_b, low_b):
+    rows = a.shape[0]
+    both = dot(jnp.concatenate([a, low], axis=0), jnp.concatenate([high_b, low_b], axis=1))
+    width = high_b.shape[1]
+    return both[:rows, :width] + both[rows:, :width] + both[:rows, width:]
+
+
+def block_inverse(lowers, span):
+    order = 2 * span
+    base = BASE // 2
+    lane = iota((base, order), 1)
+    group = (lane % span) // base
+    compact = []
+    for low in lowers:
+        halves = []
+        for j in range(2):
+            total = jnp.zeros((base, order), F32)
+            for blk in range(span // base):
+                start = j * span + blk * base
+                total = jnp.where(group == blk, low[start : start + base, :], total)
+            halves.append(total)
+        compact.append(jnp.concatenate(halves, axis=0))
+    row16, lane16 = iota((BASE, order), 0), iota((BASE, order), 1)
+    group16 = (lane16 % span) // base
+    own = (row16 % base == lane16 % base) & (row16 // base == lane16 // span)
+    inv = [own.astype(F32) for _ in lowers]
+    for s in range(BASE - 1):
+        t, j = s // 2, s % 2
+        pick = j * span + group16 * base + t
+        for n, low in enumerate(compact):
+            column = jnp.take_along_axis(low, pick, axis=1, mode="promise_in_bounds")
+            inv[n] = inv[n] - column * inv[n][j * base + t : j * base + t + 1, :]
+    tok_r = iota((order, order), 0) % span
+    tok_c = iota((order, order), 1) % span
+    pieces = [split(low) for low in lowers]
+    width = base
+    zero = jnp.zeros((), BF16)
+    while width < span:
+        diagonal = tok_r // width == tok_c // width
+        corner = (tok_r // (2 * width) == tok_c // (2 * width)) & (tok_r // width != tok_c // width)
+        second = ((iota((2 * width, order), 1) % span) // width) % 2 == 1
+        odd = [jnp.where(second, t, 0.0) for t in inv]
+        half = []
+        for t, (high, low) in zip(odd, pieces):
+            th, tl = split(t)
+            half.append(
+                pair_dot(th, tl, jnp.where(corner, high, zero), jnp.where(corner, low, zero))
+            )
+        fill = []
+        for t, y in zip(inv, half):
+            yh, yl = split(y)
+            wide = []
+            for j in range(2):
+                part = t[j * width : (j + 1) * width]
+                if width < 16:
+                    part = jnp.concatenate([part] * (16 // width), axis=0)
+                ph, pl_ = split(part)
+                count = span // part.shape[0]
+                wide.append(([ph] * count, [pl_] * count))
+            full_h = jnp.concatenate(wide[0][0] + wide[1][0], axis=0)
+            full_l = jnp.concatenate(wide[0][1] + wide[1][1], axis=0)
+            fill.append(
+                pair_dot(yh, yl, jnp.where(diagonal, full_h, zero), jnp.where(diagonal, full_l, zero))
+            )
+        merged = []
+        for t, o, r in zip(inv, odd, fill):
+            even, lower = t - o, o - r
+            merged.append(
+                jnp.concatenate(
+                    [even[:width], lower[:width], even[width:], lower[width:]], axis=0
+                )
+            )
+        inv = merged
+        width *= 2
+    return inv
+
+
+def prepare(blocks, span):
+    order = 2 * span
+    row, col = iota((order, order), 0), iota((order, order), 1)
+    tok_r, tok_c = row % span, col % span
+    strict = (tok_c < tok_r) | ((tok_c == tok_r) & (col < row))
+    eye = row == col
+    grams = [dot_t(key, key) for key, _, _ in blocks]
+    squares = jnp.concatenate(
+        [jnp.sum(jnp.where(eye, g, 0.0), axis=0, keepdims=True) for g in grams], axis=0
+    )
+    beta = jnp.concatenate([b for _, _, b in blocks], axis=0)
+    norm = lax.rsqrt(squares + 1e-06)
+    value_weight = beta * norm
+    weight = value_weight * norm
+    weight_cols = weight.T
+    lowers = [
+        jnp.where(strict, weight_cols[:, n : n + 1] * g, 0.0) for n, g in enumerate(grams)
+    ]
+    solved = block_inverse(lowers, span)
+    results = []
+    for n, (key, value, _) in enumerate(blocks):
+        th, tl = split(solved[n] * weight[n : n + 1])
+        tv = (solved[n] * value_weight[n : n + 1]).astype(BF16)
+        turn = dot(jnp.concatenate([th, tl], axis=1), jnp.concatenate([key, key], axis=0))
+        write = dot(tv, value)
+        ah, al = split(turn)
+        bh, bl = split(write)
+        stack = jnp.concatenate(
+            [jnp.concatenate([ah, bh], axis=1), jnp.concatenate([al, bl], axis=1)], axis=0
+        )
+        key_t = key.T
+        change = dot(jnp.concatenate([key_t, key_t], axis=1), stack)
+        transit = jnp.where(eye, 1.0, 0.0) - change[:, :HEAD_DIM]
+        results.append((stack, split(transit), change[:, HEAD_DIM:]))
+    return results
+
+
+def fused_kernel(
+    seq_axis, peers, axis, q_hbm, k_hbm, v_hbm, b_ref, g_hbm, w_hbm, y_hbm,
+    q_ref, k_ref, v_ref, g_ref, beta_ref, stack_ref, turn_ref, source_ref, x_ref, start_ref,
+    maps, held, carry_ref, states, s_ref, o_ref, m_ref,
+    mixed, weight, total, far_out, far_in, near_out, near_in, cross_out, cross_in, y_ref,
+    kv_sem, q_sem, g_sem, load_sem, y_sem, map_send, map_recv, back_send, back_recv,
+    far_send, far_recv, near_send, near_recv, cross_send, cross_recv,
+):
+    heads, blocks, span = q_ref.shape[0], q_ref.shape[1], q_ref.shape[2]
+    pairs = heads // 2
+    parts = 2
+    batch = blocks // parts
+    seq = lax.axis_index(seq_axis)
     me = lax.axis_index(axis)
-    heads = maps_ref.shape[0] // peers
-
-    def outward(away):
-        peer = lax.rem(me + away, peers)
+    chip, core = me // 2, me % 2
+    sibling = 2 * chip + 1 - core
+    across = 2 * (1 - chip) + core
+    beyond = 2 * (1 - chip) + 1 - core
+    width = y_ref.shape[1]
+    rows = y_ref.shape[0] // PIECES
+
+    barrier = pltpu.get_barrier_semaphore()
+    for other in (sibling, across):
+        pl.semaphore_signal(barrier, inc=1, device_id={axis: other}, device_id_type=MESH)
+    for away in range(1, peers):
+        pl.semaphore_signal(
+            barrier,
+            inc=1,
+            device_id={seq_axis: lax.rem(seq + away, peers)},
+            device_id_type=MESH,
+        )
+
+    def columns(h):
+        return pl.ds(pl.multiple_of(h * HEAD_DIM, HEAD_DIM), HEAD_DIM)
+
+    def fetch_kv(h):
+        return (
+            pltpu.make_async_copy(k_hbm.at[:, :, :, columns(h)], k_ref.at[h], kv_sem.at[0, h]),
+            pltpu.make_async_copy(v_hbm.at[:, :, :, columns(h)], v_ref.at[h], kv_sem.at[1, h]),
+        )
+
+    def fetch_q(h):
+        return pltpu.make_async_copy(q_hbm.at[:, :, columns(h)], q_ref.at[h], q_sem.at[h])
+
+    def fetch_g(h):
+        return pltpu.make_async_copy(g_hbm.at[:, :, columns(h)], g_ref.at[h], g_sem.at[h])
+
+    def load(n):
+        owner = (beyond, across, sibling, me)[n]
+        return pltpu.make_async_copy(
+            w_hbm.at[:, pl.ds(pl.multiple_of(owner * width, width), width)],
+            weight.at[n],
+            load_sem.at[n],
+        )
+
+    for h in range(heads):
+        for copy in fetch_kv(h):
+            copy.start()
+    for h in range(heads):
+        fetch_q(h).start()
+    for blk in range(blocks):
+        window = slice(blk * span, (blk + 1) * span)
+        beta_ref[blk] = jnp.concatenate([b_ref[:, 0, window], b_ref[:, 1, window]], axis=1)
+    begin = (iota((HEAD_DIM, 2 * HEAD_DIM), 0) == iota((HEAD_DIM, 2 * HEAD_DIM), 1)).astype(F32)
+    for h in range(heads + 2):
+        x_ref[h] = begin
+    for n in range(2 * batch):
+        turn_ref[1, n] = jnp.zeros((HEAD_DIM, 2 * HEAD_DIM), BF16)
+        source_ref[1, n] = jnp.zeros((HEAD_DIM, HEAD_DIM), F32)
+
+    def solve(it):
+        pair, part = it // parts, it % parts
+        work = []
+        for b in range(batch):
+            for i in range(2):
+                h = 2 * pair + i
+                blk = part * batch + b
+                key = jnp.concatenate([k_ref[h, 0, blk], k_ref[h, 1, blk]], axis=0)
+                value = jnp.concatenate([v_ref[h, 0, blk], v_ref[h, 1, blk]], axis=0)
+                work.append((key, value, beta_ref[blk, pl.ds(h, 1), :]))
+        for n, (stack, (th, tl), source) in enumerate(prepare(work, span)):
+            b, i = n // 2, n % 2
+            stack_ref[2 * pair + i, part * batch + b] = stack
+            turn_ref[it % 2, n] = jnp.concatenate([th, tl], axis=1)
+            source_ref[it % 2, n] = source
+
+    def compose(it, pair, part):
+        states_now = [x_ref[2 * pair + i] for i in range(2)]
+        for b in range(batch):
+            for i in range(2):
+                n = 2 * b + i
+                high, low = split(states_now[i])
+                start_ref[2 * pair + i, part * batch + b] = high
+                both = turn_ref[it % 2, n]
+                moved = dot(
+                    jnp.concatenate([both, both[:, :HEAD_DIM]], axis=1),
+                    jnp.concatenate([high, high, low], axis=0),
+                )
+                states_now[i] = jnp.concatenate(
+                    [moved[:, :HEAD_DIM], moved[:, HEAD_DIM:] + source_ref[it % 2, n]], axis=1
+                )
+        for i in range(2):
+            x_ref[2 * pair + i] = states_now[i]
+
+    def owner_of(pair, i):
+        side = lax.rem(pair + core, 2)
+        return peers // 2 - 2 + side + i * (3 - 2 * side)
+
+    def send_map(pair, i, source):
+        h = 2 * pair + i
         return pltpu.make_async_remote_copy(
-            src_ref=maps_ref.at[pl.ds(peer * heads, heads)],
-            dst_ref=held.at[pl.ds(me * heads, heads)],
-            send_sem=out_send.at[away],
-            recv_sem=out_recv.at[away],
-            device_id={axis: peer},
+            src_ref=maps.at[h],
+            dst_ref=held.at[pair, source],
+            send_sem=map_send.at[h],
+            recv_sem=map_recv.at[pair, source],
+            device_id={seq_axis: owner_of(pair, i)},
             device_id_type=MESH,
         )
 
-    def homeward(away):
-        peer = lax.rem(me + away, peers)
+    def send_state(pair, i, target):
+        h = 2 * pair + i
         return pltpu.make_async_remote_copy(
-            src_ref=states.at[pl.ds(peer * heads, heads)],
-            dst_ref=own_ref.at[pl.ds(me * heads, heads)],
-            send_sem=back_send.at[away],
-            recv_sem=back_recv.at[away],
-            device_id={axis: peer},
+            src_ref=states.at[pair, target],
+            dst_ref=s_ref.at[h],
+            send_sem=back_send.at[pair, target],
+            recv_sem=back_recv.at[h],
+            device_id={seq_axis: target},
             device_id_type=MESH,
         )
 
-    for away in range(1, peers):
-        outward(away).start()
-    for h in range(heads):
-        held[me * heads + h] = maps_ref[me * heads + h]
-    for away in range(1, peers):
-        outward(away).wait()
-    chain_kernel(peers, held, states)
-    for away in range(1, peers):
-        homeward(away).start()
-    for h in range(heads):
-        own_ref[me * heads + h] = states[me * heads + h]
-    for away in range(1, peers):
-        homeward(away).wait()
+    def post(pair):
+        for i in range(2):
+            h = 2 * pair + i
+            maps[h] = x_ref[h].astype(BF16)
+
+            @pl.when((seq != owner_of(pair, i)) & (seq != peers - 1))
+            def _():
+                send_map(pair, i, seq).start()
+
+            @pl.when(seq == owner_of(pair, i))
+            def _():
+                held[pair, seq] = maps[h]
+
+    def chain(pair):
+        for i in range(2):
+
+            @pl.when(seq == owner_of(pair, i))
+            def _():
+                carry_ref[...] = jnp.zeros((HEAD_DIM, HEAD_DIM), F32)
+                for k in range(peers - 1):
+
+                    @pl.when(seq != k)
+                    def _():
+                        send_map(pair, i, k).wait_recv()
+
+                    here = held[pair, k]
+                    high, low = split(carry_ref[...])
+                    turn = here[:, :HEAD_DIM]
+                    state = here[:, HEAD_DIM:].astype(F32) + dot(
+                        jnp.concatenate([turn, turn], axis=1),
+                        jnp.concatenate([high, low], axis=0),
+                    )
+                    carry_ref[...] = state
+                    states[pair, k + 1] = state.astype(BF16)
+
+                    @pl.when(seq != k + 1)
+                    def _():
+                        send_state(pair, i, k + 1).start()
+
+                    @pl.when(seq == k + 1)
+                    def _():
+                        s_ref[2 * pair + i] = states[pair, k + 1]
+
+    @pl.when(seq == 0)
+    def _():
+        s_ref[...] = jnp.zeros(s_ref.shape, BF16)
+
+    def step(it, _):
+        @pl.when(it % parts == 0)
+        def _():
+            for i in range(2):
+                for copy in fetch_kv(2 * (it // parts) + i):
+                    copy.wait()
+
+        before = it + parts * pairs
+        slot = jnp.where(it == 0, pairs, (it - 1 + parts) // parts - 1)
+        compose(it + 1, slot, (it + parts - 1) % parts)
+        solve(it)
+
+        @pl.when(it == 1)
+        def _():
+            for n in range(4):
+                load(n).start()
+            for h in range(heads):
+                fetch_g(h).start()
+
+        @pl.when(it == parts)
+        def _():
+            pl.semaphore_wait(barrier, peers + 1)
+
+        @pl.when((it % parts == 0) & (it > 0))
+        def _():
+            post(it // parts - 1)
+
+        @pl.when(it == parts * pairs - 2)
+        def _():
+            chain(0)
+
+        return 0
+
+    lax.fori_loop(0, parts * pairs, step, 0)
+    compose(parts * pairs + 1, pairs - 1, parts - 1)
+    post(pairs - 1)
+    for h in range(heads):
+        fetch_q(h).wait()
+
+    def read(pair, _):
+        causal = iota((span, 2 * span), 1) % span <= iota((span, 2 * span), 0)
+        for i in range(2):
+            h = 2 * pair + i
+            scores = []
+            for blk in range(blocks):
+                key = jnp.concatenate([k_ref[h, 0, blk], k_ref[h, 1, blk]], axis=0)
+                found = jnp.where(causal, dot_t(q_ref[h, blk], key), 0.0).astype(BF16)
+                scores.append(jnp.concatenate([found, found], axis=1))
+            drawn = [dot(score, stack_ref[h, blk]) for blk, score in enumerate(scores)]
+            for blk in range(blocks):
+                kept = (q_ref[h, blk].astype(F32) - drawn[blk][:, :HEAD_DIM]).astype(BF16)
+                out = dot(kept, start_ref[h, blk])
+                m_ref[h, blk] = out[:, :HEAD_DIM].astype(BF16)
+                o_ref[h, blk] = out[:, HEAD_DIM:] + drawn[blk][:, HEAD_DIM:]
+
+        @pl.when(pair != 1)
+        def _():
+            chain(jnp.maximum(pair, 1))
+
+        return 0
+
+    lax.fori_loop(0, pairs, read, 0)
+    for pair in range(pairs):
+        for i in range(2):
+
+            @pl.when((seq != owner_of(pair, i)) & (seq != 0))
+            def _():
+                send_state(pair, i, seq).wait_recv()
+
+    for h in range(heads):
+        fetch_g(h).wait()
+
+    def send(source, target, send_sem, recv_sem, t, device):
+        return pltpu.make_async_remote_copy(
+            src_ref=source.at[t],
+            dst_ref=target.at[t],
+            send_sem=send_sem.at[t],
+            recv_sem=recv_sem.at[t],
+            device_id={axis: device},
+            device_id_type=MESH,
+        )
+
+    def far(t):
+        return send(far_out, far_in, far_send, far_recv, t, sibling)
+
+    def near(t):
+        return send(near_out, near_in, near_send, near_recv, t, sibling)
+
+    def cross(t):
+        return send(cross_out, cross_in, cross_send, cross_recv, t, across)
+
+    def pass_on(t):
+        far(t).wait()
+        cross_out[t] = (total[t] + far_in[t].astype(F32)).astype(BF16)
+        cross(t).start()
+
+    def blend(t):
+        count = rows // span
+        for h in range(heads):
+            window = slice(t * count, (t + 1) * count)
+            query = q_ref[h, window].reshape(rows, HEAD_DIM).astype(F32)
+            unit = lax.rsqrt(jnp.sum(query * query, axis=1, keepdims=True) + 1e-06)
+            seen = o_ref[h, window].reshape(rows, HEAD_DIM) + dot(
+                m_ref[h, window].reshape(rows, HEAD_DIM), s_ref[h]
+            )
+            seen = unit * seen
+            scale = lax.rsqrt(jnp.mean(seen * seen, axis=1, keepdims=True) + 1e-06)
+            gate = g_ref[h, window].reshape(rows, HEAD_DIM).astype(F32)
+            mixed[t, :, h * HEAD_DIM : (h + 1) * HEAD_DIM] = (
+                seen * scale * (gate / (1.0 + jnp.exp(-gate)))
+            ).astype(BF16)
+
+    for t in range(PIECES):
+        blend(t)
+        if t == 0:
+            load(0).wait()
+        far_out[t] = dot(mixed[t], weight[0]).astype(BF16)
+        far(t).start()
+        if t == 0:
+            load(1).wait()
+        total[t] = dot(mixed[t], weight[1])
+        if t > 0:
+            pass_on(t - 1)
+    load(2).wait()
+    for t in range(PIECES):
+        near_out[t] = dot(mixed[t], weight[2]).astype(BF16)
+        near(t).start()
+        if t == 0:
+            pass_on(PIECES - 1)
+    load(3).wait()
+    for t in range(PIECES):
+        total[t] = dot(mixed[t], weight[3])
+
+    def put(t):
+        span_t = pl.ds(t * rows, rows)
+        return pltpu.make_async_copy(y_ref.at[span_t], y_hbm.at[span_t], y_sem.at[t])
+
+    for t in range(PIECES):
+        near(t).wait()
+        cross(t).wait()
+        y_ref[t * rows : (t + 1) * rows, :] = (
+            total[t] + near_in[t].astype(F32) + cross_in[t].astype(F32)
+        ).astype(BF16)
+        put(t).start()
+    for pair in range(pairs):
+        for i in range(2):
+
+            @pl.when((seq != owner_of(pair, i)) & (seq != peers - 1))
+            def _():
+                send_map(pair, i, seq).wait_send()
+
+            @pl.when(seq == owner_of(pair, i))
+            def _():
+                for k in range(1, peers):
+
+                    @pl.when(seq != k)
+                    def _():
+                        send_state(pair, i, k).wait_send()
+
+    for t in range(PIECES):
+        put(t).wait()
+
+
+def fused(queries, keys, values, betas, gate, out_weight, seq_axis, axis):
+    tokens, depth = queries.shape
+    heads = depth // HEAD_DIM
+    peers = lax.axis_size(seq_axis)
+    width = out_weight.shape[1] // lax.axis_size(axis)
+    blocks = tokens // SPAN
+    batch = blocks // 2
+    vmem = pl.BlockSpec(memory_space=pltpu.VMEM)
+    hbm = pl.BlockSpec(memory_space=pl.ANY)
+    piece = (PIECES, tokens // PIECES, width)
+    square = (HEAD_DIM, HEAD_DIM)
+    wide = (HEAD_DIM, 2 * HEAD_DIM)
+    pairs = heads // 2
+    dma = pltpu.SemaphoreType.DMA
+    per_head = (heads, blocks, SPAN, HEAD_DIM)
+    both = (heads, 2, blocks, SPAN, HEAD_DIM)
+    return pl.pallas_call(
+        functools.partial(fused_kernel, seq_axis, peers, axis),
+        in_specs=[hbm, hbm, hbm, vmem, hbm, hbm],
+        out_specs=hbm,
+        out_shape=jax.ShapeDtypeStruct((tokens, width), BF16),
+        scratch_shapes=[
+            pltpu.VMEM(per_head, BF16),
+            pltpu.VMEM(both, BF16),
+            pltpu.VMEM(both, BF16),
+            pltpu.VMEM(per_head, BF16),
+            pltpu.VMEM((blocks, heads, 2 * SPAN), F32),
+            pltpu.VMEM((heads, blocks, 4 * SPAN, 2 * HEAD_DIM), BF16),
+            pltpu.VMEM((2, 2 * batch) + wide, BF16),
+            pltpu.VMEM((2, 2 * batch) + square, F32),
+            pltpu.VMEM((heads + 2,) + wide, F32),
+            pltpu.VMEM((heads + 2, blocks) + wide, BF16),
+            pltpu.VMEM((heads,) + wide, BF16),
+            pltpu.VMEM((pairs, peers) + wide, BF16),
+            pltpu.VMEM(square, F32),
+            pltpu.VMEM((pairs, peers) + square, BF16),
+            pltpu.VMEM((heads,) + square, BF16),
+            pltpu.VMEM(per_head, F32),
+            pltpu.VMEM(per_head, BF16),
+            pltpu.VMEM((PIECES, tokens // PIECES, depth), BF16),
+            pltpu.VMEM((4, depth, width), BF16),
+            pltpu.VMEM(piece, F32),
+        ]
+        + [pltpu.VMEM(piece, BF16)] * 6
+        + [
+            pltpu.VMEM((tokens, width), BF16),
+            dma((2, heads)),
+            dma((heads,)),
+            dma((heads,)),
+            dma((4,)),
+            dma((PIECES,)),
+            dma((heads,)),
+            dma((pairs, peers)),
+            dma((pairs, peers)),
+            dma((heads,)),
+        ]
+        + [dma((PIECES,))] * 6,
+        compiler_params=pltpu.CompilerParams(
+            collective_id=0, has_side_effects=True, vmem_limit_bytes=VMEM_LIMIT
+        ),
+    )(
+        queries.reshape(blocks, SPAN, depth),
+        keys.reshape(2, blocks, SPAN, depth),
+        values.reshape(2, blocks, SPAN, depth),
+        betas,
+        gate.reshape(blocks, SPAN, depth),
+        out_weight,
+    )
 
 
 def start_state(maps, axis):
@@ -241,147 +728,6 @@
         compiler_params=pltpu.CompilerParams(vmem_limit_bytes=VMEM_LIMIT),
     )(held)
     return lax.dynamic_slice_in_dim(states, index * heads, heads, 0)
-
-
-def finish_kernel(
-    seq_axis, seq_peers, axis, maps_ref, o_hbm, m_hbm, g_hbm, w_ref, y_ref,
-    held, states, s_ref, o_ref, m_ref, g_ref,
-    mixed, weight, total, far_out, far_in, near_out, near_in, cross_out, cross_in,
-    out_send, out_recv, back_send, back_recv, fetch_sem,
-    load_sem, far_send, far_recv, near_send, near_recv, cross_send, cross_recv,
-):
-    me = lax.axis_index(axis)
-    chip, core = me // 2, me % 2
-    sibling = 2 * chip + 1 - core
-    across = 2 * (1 - chip) + core
-    beyond = 2 * (1 - chip) + 1 - core
-    width = y_ref.shape[1]
-    rows = y_ref.shape[0] // PIECES
-
-    fetches = [
-        pltpu.make_async_copy(source, target, fetch_sem.at[n])
-        for n, (source, target) in enumerate(((o_hbm, o_ref), (m_hbm, m_ref), (g_hbm, g_ref)))
-    ]
-    loads = []
-    for n, owner in enumerate((beyond, across, sibling, me)):
-        loads.append(
-            pltpu.make_async_copy(
-                w_ref.at[:, pl.ds(pl.multiple_of(owner * width, width), width)],
-                weight.at[n],
-                load_sem.at[n],
-            )
-        )
-
-    barrier = pltpu.get_barrier_semaphore()
-    for other in (sibling, across):
-        pl.semaphore_signal(barrier, inc=1, device_id={axis: other}, device_id_type=MESH)
-    for away in range(1, seq_peers):
-        pl.semaphore_signal(
-            barrier,
-            inc=1,
-            device_id={seq_axis: lax.rem(lax.axis_index(seq_axis) + away, seq_peers)},
-            device_id_type=MESH,
-        )
-    for copy in fetches + loads:
-        copy.start()
-    pl.semaphore_wait(barrier, seq_peers + 1)
-    exchange(
-        seq_axis, seq_peers, maps_ref, s_ref, held, states, out_send, out_recv, back_send, back_recv
-    )
-    for copy in fetches:
-        copy.wait()
-
-    def send(source, target, send_sem, recv_sem, t, device):
-        return pltpu.make_async_remote_copy(
-            src_ref=source.at[t],
-            dst_ref=target.at[t],
-            send_sem=send_sem.at[t],
-            recv_sem=recv_sem.at[t],
-            device_id={axis: device},
-            device_id_type=MESH,
-        )
-
-    def far(t):
-        return send(far_out, far_in, far_send, far_recv, t, sibling)
-
-    def near(t):
-        return send(near_out, near_in, near_send, near_recv, t, sibling)
-
-    def cross(t):
-        return send(cross_out, cross_in, cross_send, cross_recv, t, across)
-
-    def pass_on(t):
-        far(t).wait()
-        cross_out[t] = (total[t] + far_in[t].astype(F32)).astype(BF16)
-        cross(t).start()
-
-    for t in range(PIECES):
-        span = slice(t * rows, (t + 1) * rows)
-        for h in range(s_ref.shape[0]):
-            cols = slice(h * HEAD_DIM, (h + 1) * HEAD_DIM)
-            seen = o_ref[span, cols] + dot(m_ref[span, cols], s_ref[h])
-            scale = lax.rsqrt(jnp.mean(seen * seen, axis=1, keepdims=True) + 1e-06)
-            gate = g_ref[span, cols].astype(F32)
-            mixed[t, :, cols] = (seen * scale * (gate / (1.0 + jnp.exp(-gate)))).astype(BF16)
-        if t == 0:
-            loads[0].wait()
-        far_out[t] = dot(mixed[t], weight[0]).astype(BF16)
-        far(t).start()
-        if t == 0:
-            loads[1].wait()
-        total[t] = dot(mixed[t], weight[1])
-        if t > 0:
-            pass_on(t - 1)
-    loads[2].wait()
-    for t in range(PIECES):
-        near_out[t] = dot(mixed[t], weight[2]).astype(BF16)
-        near(t).start()
-        if t == 0:
-            pass_on(PIECES - 1)
-    loads[3].wait()
-    for t in range(PIECES):
-        total[t] = dot(mixed[t], weight[3])
-    for t in range(PIECES):
-        near(t).wait()
-        cross(t).wait()
-        y_ref[t * rows : (t + 1) * rows, :] = (
-            total[t] + near_in[t].astype(F32) + cross_in[t].astype(F32)
-        ).astype(BF16)
-
-
-def finish(maps, local, reach, gate, out_weight, seq_axis, axis):
-    tokens, depth = local.shape
-    peers = lax.axis_size(seq_axis)
-    width = out_weight.shape[1] // lax.axis_size(axis)
-    vmem = pl.BlockSpec(memory_space=pltpu.VMEM)
-    hbm = pl.BlockSpec(memory_space=pl.ANY)
-    piece = (PIECES, tokens // PIECES, width)
-    states = (maps.shape[0], HEAD_DIM, HEAD_DIM)
-    return pl.pallas_call(
-        functools.partial(finish_kernel, seq_axis, peers, axis),
-        in_specs=[vmem, hbm, hbm, hbm, hbm],
-        out_specs=vmem,
-        out_shape=jax.ShapeDtypeStruct((tokens, width), BF16),
-        scratch_shapes=[
-            pltpu.VMEM(maps.shape, BF16),
-            pltpu.VMEM(states, BF16),
-            pltpu.VMEM(states, BF16),
-            pltpu.VMEM(local.shape, F32),
-            pltpu.VMEM(local.shape, BF16),
-            pltpu.VMEM(local.shape, BF16),
-            pltpu.VMEM((PIECES, tokens // PIECES, depth), BF16),
-            pltpu.VMEM((4, depth, width), BF16),
-            pltpu.VMEM(piece, F32),
-        ]
-        + [pltpu.VMEM(piece, BF16)] * 6
-        + [pltpu.SemaphoreType.DMA((peers,))] * 4
-        + [pltpu.SemaphoreType.DMA((3,))]
-        + [pltpu.SemaphoreType.DMA((4,))]
-        + [pltpu.SemaphoreType.DMA((PIECES,))] * 6,
-        compiler_params=pltpu.CompilerParams(
-            collective_id=0, has_side_effects=True, vmem_limit_bytes=VMEM_LIMIT
-        ),
-    )(maps, local, reach, gate, out_weight)
 
 
 def out_kernel(o_ref, m_ref, s_ref, g_ref, w_ref, y_ref, mixed_ref):
@@ -423,10 +769,11 @@
 
 def per_device(queries, keys, values, betas, gate, out_weight):
     heads, _, tokens = betas.shape
+    peers, index = lax.axis_size("ctx"), lax.axis_size("head")
+    if index == 4 and peers >= 4 and peers % 2 == 0 and heads % 8 == 0 and tokens % (8 * SPAN) == 0:
+        return fused(queries, keys, values, betas, gate, out_weight, "ctx", "head")
     beta_cols = betas.transpose(2, 1, 0).reshape(2 * tokens, heads)
     local, reach, maps = mix(queries, keys, values, beta_cols)
-    if lax.axis_size("head") == 4 and heads % lax.axis_size("ctx") == 0:
-        return finish(maps, local, reach, gate, out_weight, "ctx", "head")
     states = start_state(maps, "ctx")
     partial_sum = project(local, reach, states, gate, out_weight)
     return lax.psum_scatter(partial_sum, "head", scatter_dimension=1, tiled=True)

time: 90 us -> 79 us (0.88); the launches traced: 88.5 us -> 78.5 us
  Pallas kernels: 84.4 us -> 76.3 us
  local copies, waits for them, and re-layouts: 4.02 us -> 2.26 us
    pallas_call x2 -> x1, Pallas kernels: 84.4 us -> 76.3 us  [fused(): pl.pallas_call(functools.partial(fused_kernel, seq_axis, peers, axis), in...]
    transpose x1 -> x0, local copies, waits for them, and re-layouts: 1.76 us -> none  [per_device(): beta_cols = betas.transpose(2, 1, 0).reshape(2 * tokens, heads)]
where the time goes in v1:
time: 79 us; the launch traced here: 78.5 us
  Pallas kernels  76.3 us (97%)
  local copies, waits for them, and re-layouts  2.26 us (3%)
    pallas_call x1, Pallas kernels, fused(): pl.pallas_call(functools.partial(fused_kernel, seq_axis, peers, axis), in...  76.3 us
    unnamed x1, local copies, waits for them, and re-layouts  2.26 us

profile of v1, /device:TPU:24, one launch (start us, length us, event | category | flops | bytes accessed | tf_op | source)
XLA Modules:
  0.0 78.5 jit_solution(7930453032507712028)
XLA Ops:
  0.0 76.3 %shard_map.64 = bf16[512,1024]{1,0:T(8,128)(2,1)} custom-call(bf16[8,64,1024]{2,1,0:T(8,128)(2,1)} %bitcast.6, bf16[2,8,64,1024]{3,2,1,0:T(8,128)(2,1)} %bitcast.4, bf16[2,8,64,1024]{3,2,1,0:T(8,128)(2,1)} %bitcast.5, f32[8,2,512]{2,1,0:T(2,128)} %b_ref.1, bf16[8,64,1024]{2,1,0:T(8,128)(2,1)} %bitcast.7, bf16[1024,4096]{1,0:T(8,128)(2,1)} %w_hbm.1), custom_call_target="tpu_custom_call" | custom-call | tf_op jit(solution)/shard_map/pallas_call | solution.py:667
  76.3 2.3 %copy.8 = bf16[512,1024]{1,0:T(8,128)(2,1)} copy(bf16[512,1024]{1,0:T(8,128)(2,1)} %shard_map.64) | data formatting | bytes 2097152

commit v2 on v1

--- a/solution.py
+++ b/solution.py
@@ -201,7 +201,18 @@
     return both[:rows, :width] + both[rows:, :width] + both[:rows, width:]
 
 
-def block_inverse(lowers, span):
+def weave(*streams):
+    order = []
+    for n, (count, _) in enumerate(streams):
+        order += [((k + 0.5) / count, n) for k in range(count)]
+    for _, n in sorted(order):
+        next(streams[n][1], None)
+    for _, stream in streams:
+        for _ in stream:
+            pass
+
+
+def base_solve(lowers, span):
     order = 2 * span
     base = BASE // 2
     lane = iota((base, order), 1)
@@ -216,6 +227,7 @@
                 total = jnp.where(group == blk, low[start : start + base, :], total)
             halves.append(total)
         compact.append(jnp.concatenate(halves, axis=0))
+        yield
     row16, lane16 = iota((BASE, order), 0), iota((BASE, order), 1)
     group16 = (lane16 % span) // base
     own = (row16 % base == lane16 % base) & (row16 // base == lane16 // span)
@@ -226,39 +238,50 @@
         for n, low in enumerate(compact):
             column = jnp.take_along_axis(low, pick, axis=1, mode="promise_in_bounds")
             inv[n] = inv[n] - column * inv[n][j * base + t : j * base + t + 1, :]
+        yield
+    return inv
+
+
+def merge(inv, pieces, span):
+    order = 2 * span
     tok_r = iota((order, order), 0) % span
     tok_c = iota((order, order), 1) % span
-    pieces = [split(low) for low in lowers]
-    width = base
+    width = BASE // 2
     zero = jnp.zeros((), BF16)
     while width < span:
+        last = 2 * width == span
         diagonal = tok_r // width == tok_c // width
         corner = (tok_r // (2 * width) == tok_c // (2 * width)) & (tok_r // width != tok_c // width)
         second = ((iota((2 * width, order), 1) % span) // width) % 2 == 1
-        odd = [jnp.where(second, t, 0.0) for t in inv]
-        half = []
-        for t, (high, low) in zip(odd, pieces):
-            th, tl = split(t)
-            half.append(
-                pair_dot(th, tl, jnp.where(corner, high, zero), jnp.where(corner, low, zero))
-            )
-        fill = []
-        for t, y in zip(inv, half):
-            yh, yl = split(y)
-            wide = []
+        odd, half, fill, wide, merged = [], [], [], [], []
+        for n, t in enumerate(inv):
+            odd.append(jnp.where(second, t, 0.0))
+            th, tl = split(odd[n])
+            high, low = pieces(n)
+            if last:
+                y = jnp.where(second, 0.0, pair_dot(th, tl, high, low))
+            else:
+                y = pair_dot(th, tl, jnp.where(corner, high, zero), jnp.where(corner, low, zero))
+            half.append(y)
+            parts = []
             for j in range(2):
                 part = t[j * width : (j + 1) * width]
                 if width < 16:
                     part = jnp.concatenate([part] * (16 // width), axis=0)
-                ph, pl_ = split(part)
-                count = span // part.shape[0]
-                wide.append(([ph] * count, [pl_] * count))
-            full_h = jnp.concatenate(wide[0][0] + wide[1][0], axis=0)
-            full_l = jnp.concatenate(wide[0][1] + wide[1][1], axis=0)
-            fill.append(
-                pair_dot(yh, yl, jnp.where(diagonal, full_h, zero), jnp.where(diagonal, full_l, zero))
-            )
-        merged = []
+                parts.append((split(part), span // part.shape[0]))
+            full = [
+                jnp.concatenate([p[k] for p, count in parts for _ in range(count)], axis=0)
+                for k in range(2)
+            ]
+            if not last:
+                full = [jnp.where(diagonal, f, zero) for f in full]
+            wide.append(full)
+            yield
+        for y, full in zip(half, wide):
+            yh, yl = split(y)
+            r = pair_dot(yh, yl, full[0], full[1])
+            fill.append(jnp.where(second, 0.0, r) if last else r)
+            yield
         for t, o, r in zip(inv, odd, fill):
             even, lower = t - o, o - r
             merged.append(
@@ -271,46 +294,10 @@
     return inv
 
 
-def prepare(blocks, span):
-    order = 2 * span
-    row, col = iota((order, order), 0), iota((order, order), 1)
-    tok_r, tok_c = row % span, col % span
-    strict = (tok_c < tok_r) | ((tok_c == tok_r) & (col < row))
-    eye = row == col
-    grams = [dot_t(key, key) for key, _, _ in blocks]
-    squares = jnp.concatenate(
-        [jnp.sum(jnp.where(eye, g, 0.0), axis=0, keepdims=True) for g in grams], axis=0
-    )
-    beta = jnp.concatenate([b for _, _, b in blocks], axis=0)
-    norm = lax.rsqrt(squares + 1e-06)
-    value_weight = beta * norm
-    weight = value_weight * norm
-    weight_cols = weight.T
-    lowers = [
-        jnp.where(strict, weight_cols[:, n : n + 1] * g, 0.0) for n, g in enumerate(grams)
-    ]
-    solved = block_inverse(lowers, span)
-    results = []
-    for n, (key, value, _) in enumerate(blocks):
-        th, tl = split(solved[n] * weight[n : n + 1])
-        tv = (solved[n] * value_weight[n : n + 1]).astype(BF16)
-        turn = dot(jnp.concatenate([th, tl], axis=1), jnp.concatenate([key, key], axis=0))
-        write = dot(tv, value)
-        ah, al = split(turn)
-        bh, bl = split(write)
-        stack = jnp.concatenate(
-            [jnp.concatenate([ah, bh], axis=1), jnp.concatenate([al, bl], axis=1)], axis=0
-        )
-        key_t = key.T
-        change = dot(jnp.concatenate([key_t, key_t], axis=1), stack)
-        transit = jnp.where(eye, 1.0, 0.0) - change[:, :HEAD_DIM]
-        results.append((stack, split(transit), change[:, HEAD_DIM:]))
-    return results
-
-
 def fused_kernel(
     seq_axis, peers, axis, q_hbm, k_hbm, v_hbm, b_ref, g_hbm, w_hbm, y_hbm,
     q_ref, k_ref, v_ref, g_ref, beta_ref, stack_ref, turn_ref, source_ref, x_ref, start_ref,
+    low_ref, inv_ref, weight_ref, eye_ref,
     maps, held, carry_ref, states, s_ref, o_ref, m_ref,
     mixed, weight, total, far_out, far_in, near_out, near_in, cross_out, cross_in, y_ref,
     kv_sem, q_sem, g_sem, load_sem, y_sem, map_send, map_recv, back_send, back_recv,
@@ -372,45 +359,118 @@
         window = slice(blk * span, (blk + 1) * span)
         beta_ref[blk] = jnp.concatenate([b_ref[:, 0, window], b_ref[:, 1, window]], axis=1)
     begin = (iota((HEAD_DIM, 2 * HEAD_DIM), 0) == iota((HEAD_DIM, 2 * HEAD_DIM), 1)).astype(F32)
-    for h in range(heads + 2):
+    for h in range(heads):
         x_ref[h] = begin
-    for n in range(2 * batch):
-        turn_ref[1, n] = jnp.zeros((HEAD_DIM, 2 * HEAD_DIM), BF16)
-        source_ref[1, n] = jnp.zeros((HEAD_DIM, HEAD_DIM), F32)
+    eye_ref[...] = (iota(eye_ref.shape, 0) == iota(eye_ref.shape, 1)).astype(F32)
+
+    def place(it, n):
+        pair, part = it // parts, it % parts
+        return 2 * pair + n % 2, part * batch + n // 2
+
+    count = 2 * batch
+
+    def key_of(h, blk):
+        return jnp.concatenate([k_ref[h, 0, blk], k_ref[h, 1, blk]], axis=0)
 
     def solve(it):
+        order = 2 * span
+        row, col = iota((order, order), 0), iota((order, order), 1)
+        tok_r, tok_c = row % span, col % span
+        strict = (tok_c < tok_r) | ((tok_c == tok_r) & (col < row))
+        slot = it % 2
+        grams, squares = [], []
+        for n in range(count):
+            key = key_of(*place(it, n))
+            grams.append(dot_t(key, key))
+            yield
+        for g in grams:
+            squares.append(jnp.sum(eye_ref[...] * g, axis=0, keepdims=True))
+            yield
+        beta = jnp.concatenate(
+            [beta_ref[place(it, n)[1], pl.ds(place(it, n)[0], 1), :] for n in range(count)], axis=0
+        )
+        norm = lax.rsqrt(jnp.concatenate(squares, axis=0) + 1e-06)
+        value_weight = beta * norm
+        weight_rows = value_weight * norm
+        weight_ref[slot, 0] = weight_rows
+        weight_ref[slot, 1] = value_weight
+        weight_cols = weight_rows.T
+        yield
+        lowers = []
+        for n, g in enumerate(grams):
+            low = jnp.where(strict, weight_cols[:, n : n + 1] * g, 0.0)
+            lowers.append(low)
+            low_ref[slot, n] = jnp.concatenate(split(low), axis=1)
+            yield
+        inv = yield from base_solve(lowers, span)
+        for n in range(count):
+            inv_ref[slot, n] = inv[n]
+
+    def transit(it):
+        slot = it % 2
+
+        def pieces(n):
+            return low_ref[slot, n, :, : 2 * span], low_ref[slot, n, :, 2 * span :]
+
+        solved = yield from merge([inv_ref[slot, n] for n in range(count)], pieces, span)
+        turns, writes, changes = [], [], []
+        for n in range(count):
+            h, blk = place(it, n)
+            th, tl = split(solved[n] * weight_ref[slot, 0, n : n + 1, :])
+            tv = (solved[n] * weight_ref[slot, 1, n : n + 1, :]).astype(BF16)
+            key = key_of(h, blk)
+            value = jnp.concatenate([v_ref[h, 0, blk], v_ref[h, 1, blk]], axis=0)
+            turns.append(
+                dot(jnp.concatenate([th, tl], axis=1), jnp.concatenate([key, key], axis=0))
+            )
+            writes.append(dot(tv, value))
+            yield
+        for n in range(count):
+            h, blk = place(it, n)
+            ah, al = split(turns[n])
+            bh, bl = split(writes[n])
+            stack = jnp.concatenate(
+                [jnp.concatenate([ah, bh], axis=1), jnp.concatenate([al, bl], axis=1)], axis=0
+            )
+            stack_ref[h, blk] = stack
+            key_t = key_of(h, blk).T
+            changes.append(dot(jnp.concatenate([key_t, key_t], axis=1), stack))
+            yield
+        for n in range(count):
+            step = eye_ref[...] - changes[n][:, :HEAD_DIM]
+            turn_ref[slot, n] = jnp.concatenate(split(step), axis=1)
+            source_ref[slot, n] = changes[n][:, HEAD_DIM:]
+            yield
+
+    def compose(it):
+        slot = it % 2
         pair, part = it // parts, it % parts
-        work = []
-        for b in range(batch):
-            for i in range(2):
-                h = 2 * pair + i
-                blk = part * batch + b
-                key = jnp.concatenate([k_ref[h, 0, blk], k_ref[h, 1, blk]], axis=0)
-                value = jnp.concatenate([v_ref[h, 0, blk], v_ref[h, 1, blk]], axis=0)
-                work.append((key, value, beta_ref[blk, pl.ds(h, 1), :]))
-        for n, (stack, (th, tl), source) in enumerate(prepare(work, span)):
-            b, i = n // 2, n % 2
-            stack_ref[2 * pair + i, part * batch + b] = stack
-            turn_ref[it % 2, n] = jnp.concatenate([th, tl], axis=1)
-            source_ref[it % 2, n] = source
-
-    def compose(it, pair, part):
         states_now = [x_ref[2 * pair + i] for i in range(2)]
-        for b in range(batch):
-            for i in range(2):
-                n = 2 * b + i
-                high, low = split(states_now[i])
-                start_ref[2 * pair + i, part * batch + b] = high
-                both = turn_ref[it % 2, n]
-                moved = dot(
-                    jnp.concatenate([both, both[:, :HEAD_DIM]], axis=1),
-                    jnp.concatenate([high, high, low], axis=0),
-                )
-                states_now[i] = jnp.concatenate(
-                    [moved[:, :HEAD_DIM], moved[:, HEAD_DIM:] + source_ref[it % 2, n]], axis=1
-                )
+        for n in range(count):
+            h, blk = place(it, n)
+            i = n % 2
+            high, low = split(states_now[i])
+            start_ref[h, blk] = high
+            both = turn_ref[slot, n]
+            moved = dot(
+                jnp.concatenate([both, both[:, :HEAD_DIM]], axis=1),
+                jnp.concatenate([high, high, low], axis=0),
+            )
+            states_now[i] = jnp.concatenate(
+                [moved[:, :HEAD_DIM], moved[:, HEAD_DIM:] + source_ref[slot, n]], axis=1
+            )
+            yield
         for i in range(2):
             x_ref[2 * pair + i] = states_now[i]
+
+    def a_stream(it):
+        return 4 * count + BASE, solve(it)
+
+    def b_stream(it):
+        return 9 * count, transit(it)
+
+    def c_stream(it):
+        return count, compose(it)
 
     def owner_of(pair, i):
         side = lax.rem(pair + core, 2)
@@ -485,41 +545,44 @@
     def _():
         s_ref[...] = jnp.zeros(s_ref.shape, BF16)
 
+    def wait_kv(pair):
+        for i in range(2):
+            for copy in fetch_kv(2 * pair + i):
+                copy.wait()
+
+    steps = parts * pairs
+    wait_kv(0)
+    weave(a_stream(0))
+    for n in range(4):
+        load(n).start()
+    for h in range(heads):
+        fetch_g(h).start()
+    weave(a_stream(1), b_stream(0))
+
     def step(it, _):
         @pl.when(it % parts == 0)
         def _():
-            for i in range(2):
-                for copy in fetch_kv(2 * (it // parts) + i):
-                    copy.wait()
-
-        before = it + parts * pairs
-        slot = jnp.where(it == 0, pairs, (it - 1 + parts) // parts - 1)
-        compose(it + 1, slot, (it + parts - 1) % parts)
-        solve(it)
-
-        @pl.when(it == 1)
-        def _():
-            for n in range(4):
-                load(n).start()
-            for h in range(heads):
-                fetch_g(h).start()
-
-        @pl.when(it == parts)
+            wait_kv(it // parts)
+
+        weave(a_stream(it), b_stream(it - 1), c_stream(it - 2))
+
+        @pl.when(it == parts + 1)
         def _():
             pl.semaphore_wait(barrier, peers + 1)
 
-        @pl.when((it % parts == 0) & (it > 0))
+        @pl.when(it % parts == 1)
         def _():
             post(it // parts - 1)
 
-        @pl.when(it == parts * pairs - 2)
+        @pl.when(it == steps - 2)
         def _():
             chain(0)
 
         return 0
 
-    lax.fori_loop(0, parts * pairs, step, 0)
-    compose(parts * pairs + 1, pairs - 1, parts - 1)
+    lax.fori_loop(2, steps, step, 0)
+    weave(b_stream(steps - 1), c_stream(steps - 2))
+    weave(c_stream(steps - 1))
     post(pairs - 1)
     for h in range(heads):
         fetch_q(h).wait()
@@ -530,8 +593,7 @@
             h = 2 * pair + i
             scores = []
             for blk in range(blocks):
-                key = jnp.concatenate([k_ref[h, 0, blk], k_ref[h, 1, blk]], axis=0)
-                found = jnp.where(causal, dot_t(q_ref[h, blk], key), 0.0).astype(BF16)
+                found = jnp.where(causal, dot_t(q_ref[h, blk], key_of(h, blk)), 0.0).astype(BF16)
                 scores.append(jnp.concatenate([found, found], axis=1))
             drawn = [dot(score, stack_ref[h, blk]) for blk, score in enumerate(scores)]
             for blk in range(blocks):
@@ -582,9 +644,9 @@
         cross(t).start()
 
     def blend(t):
-        count = rows // span
+        held_blocks = rows // span
         for h in range(heads):
-            window = slice(t * count, (t + 1) * count)
+            window = slice(t * held_blocks, (t + 1) * held_blocks)
             query = q_ref[h, window].reshape(rows, HEAD_DIM).astype(F32)
             unit = lax.rsqrt(jnp.sum(query * query, axis=1, keepdims=True) + 1e-06)
             seen = o_ref[h, window].reshape(rows, HEAD_DIM) + dot(
@@ -678,8 +740,12 @@
             pltpu.VMEM((heads, blocks, 4 * SPAN, 2 * HEAD_DIM), BF16),
             pltpu.VMEM((2, 2 * batch) + wide, BF16),
             pltpu.VMEM((2, 2 * batch) + square, F32),
-            pltpu.VMEM((heads + 2,) + wide, F32),
-            pltpu.VMEM((heads + 2, blocks) + wide, BF16),
+            pltpu.VMEM((heads,) + wide, F32),
+            pltpu.VMEM((heads, blocks) + wide, BF16),
+            pltpu.VMEM((2, 2 * batch) + wide, BF16),
+            pltpu.VMEM((2, 2 * batch, BASE, 2 * SPAN), F32),
+            pltpu.VMEM((2, 2, 2 * batch, 2 * SPAN), F32),
+            pltpu.VMEM(square, F32),
             pltpu.VMEM((heads,) + wide, BF16),
             pltpu.VMEM((pairs, peers) + wide, BF16),
             pltpu.VMEM(square, F32),

time: 79 us -> 61.6 us (0.78)
  Pallas kernels: 76.3 us -> 58.8 us
    pallas_call x1, Pallas kernels: 76.3 us -> 58.8 us  [fused(): pl.pallas_call(functools.partial(fused_kernel, seq_axis, peers, axis), in...]
where the time goes in v2:
time: 61.6 us; the launch traced here: 61 us
  Pallas kernels  58.8 us (95%)
  local copies, waits for them, and re-layouts  2.26 us (4%)
    pallas_call x1, Pallas kernels, fused(): pl.pallas_call(functools.partial(fused_kernel, seq_axis, peers, axis), in...  58.8 us
    unnamed x1, local copies, waits for them, and re-layouts  2.26 us

profile of v2, /device:TPU:24, one launch (start us, length us, event | category | flops | bytes accessed | tf_op | source)
XLA Modules:
  0.0 61.0 jit_solution(14160716557334123859)
XLA Ops:
  0.0 58.8 %shard_map.64 = bf16[512,1024]{1,0:T(8,128)(2,1)} custom-call(bf16[8,64,1024]{2,1,0:T(8,128)(2,1)} %bitcast.6, bf16[2,8,64,1024]{3,2,1,0:T(8,128)(2,1)} %bitcast.4, bf16[2,8,64,1024]{3,2,1,0:T(8,128)(2,1)} %bitcast.5, f32[8,2,512]{2,1,0:T(2,128)} %b_ref.1, bf16[8,64,1024]{2,1,0:T(8,128)(2,1)} %bitcast.7, bf16[1024,4096]{1,0:T(8,128)(2,1)} %w_hbm.1), custom_call_target="tpu_custom_call" | custom-call | tf_op jit(solution)/shard_map/pallas_call | solution.py:729
  58.8 2.3 %copy.8 = bf16[512,1024]{1,0:T(8,128)(2,1)} copy(bf16[512,1024]{1,0:T(8,128)(2,1)} %shard_map.64) | data formatting | bytes 2097152

commit v3 on v2

--- a/solution.py
+++ b/solution.py
@@ -203,11 +203,11 @@
 
 def weave(*streams):
     order = []
-    for n, (count, _) in enumerate(streams):
-        order += [((k + 0.5) / count, n) for k in range(count)]
+    for n, (count, _, first, last) in enumerate(streams):
+        order += [(first + (last - first) * (k + 0.5) / count, n) for k in range(count)]
     for _, n in sorted(order):
         next(streams[n][1], None)
-    for _, stream in streams:
+    for _, stream, _, _ in streams:
         for _ in stream:
             pass
 
@@ -217,8 +217,12 @@
     base = BASE // 2
     lane = iota((base, order), 1)
     group = (lane % span) // base
+    row16, lane16 = iota((BASE, order), 0), iota((BASE, order), 1)
+    group16 = (lane16 % span) // base
+    row_tok, lane_tok = row16 % base, lane16 % base
+    before = (lane_tok < row_tok) | ((lane_tok == row_tok) & (lane16 // span < row16 // base))
     compact = []
-    for low in lowers:
+    for n, low in enumerate(lowers):
         halves = []
         for j in range(2):
             total = jnp.zeros((base, order), F32)
@@ -226,10 +230,9 @@
                 start = j * span + blk * base
                 total = jnp.where(group == blk, low[start : start + base, :], total)
             halves.append(total)
-        compact.append(jnp.concatenate(halves, axis=0))
-        yield
-    row16, lane16 = iota((BASE, order), 0), iota((BASE, order), 1)
-    group16 = (lane16 % span) // base
+        compact.append(jnp.where(before, jnp.concatenate(halves, axis=0), 0.0))
+        if n % 2:
+            yield
     own = (row16 % base == lane16 % base) & (row16 // base == lane16 // span)
     inv = [own.astype(F32) for _ in lowers]
     for s in range(BASE - 1):
@@ -313,8 +316,7 @@
     sibling = 2 * chip + 1 - core
     across = 2 * (1 - chip) + core
     beyond = 2 * (1 - chip) + 1 - core
-    width = y_ref.shape[1]
-    rows = y_ref.shape[0] // PIECES
+    width = y_ref.shape[2]
 
     barrier = pltpu.get_barrier_semaphore()
     for other in (sibling, across):
@@ -372,20 +374,28 @@
     def key_of(h, blk):
         return jnp.concatenate([k_ref[h, 0, blk], k_ref[h, 1, blk]], axis=0)
 
+    def stack_of(h, blk):
+        none = jnp.zeros((HEAD_DIM, HEAD_DIM), BF16)
+        return jnp.concatenate(
+            [
+                jnp.concatenate([stack_ref[h, blk, 0], stack_ref[h, blk, 2]], axis=1),
+                jnp.concatenate([stack_ref[h, blk, 1], none], axis=1),
+            ],
+            axis=0,
+        )
+
     def solve(it):
-        order = 2 * span
-        row, col = iota((order, order), 0), iota((order, order), 1)
-        tok_r, tok_c = row % span, col % span
-        strict = (tok_c < tok_r) | ((tok_c == tok_r) & (col < row))
         slot = it % 2
         grams, squares = [], []
         for n in range(count):
             key = key_of(*place(it, n))
             grams.append(dot_t(key, key))
-            yield
-        for g in grams:
+            if n % 2:
+                yield
+        for n, g in enumerate(grams):
             squares.append(jnp.sum(eye_ref[...] * g, axis=0, keepdims=True))
-            yield
+            if n % 4 == 3:
+                yield
         beta = jnp.concatenate(
             [beta_ref[place(it, n)[1], pl.ds(place(it, n)[0], 1), :] for n in range(count)], axis=0
         )
@@ -398,10 +408,11 @@
         yield
         lowers = []
         for n, g in enumerate(grams):
-            low = jnp.where(strict, weight_cols[:, n : n + 1] * g, 0.0)
+            low = weight_cols[:, n : n + 1] * g
             lowers.append(low)
-            low_ref[slot, n] = jnp.concatenate(split(low), axis=1)
-            yield
+            low_ref[slot, n, 0], low_ref[slot, n, 1] = split(low)
+            if n % 2:
+                yield
         inv = yield from base_solve(lowers, span)
         for n in range(count):
             inv_ref[slot, n] = inv[n]
@@ -410,7 +421,7 @@
         slot = it % 2
 
         def pieces(n):
-            return low_ref[slot, n, :, : 2 * span], low_ref[slot, n, :, 2 * span :]
+            return low_ref[slot, n, 0], low_ref[slot, n, 1]
 
         solved = yield from merge([inv_ref[slot, n] for n in range(count)], pieces, span)
         turns, writes, changes = [], [], []
@@ -427,18 +438,16 @@
             yield
         for n in range(count):
             h, blk = place(it, n)
-            ah, al = split(turns[n])
-            bh, bl = split(writes[n])
-            stack = jnp.concatenate(
-                [jnp.concatenate([ah, bh], axis=1), jnp.concatenate([al, bl], axis=1)], axis=0
-            )
-            stack_ref[h, blk] = stack
+            turn_h, turn_l = split(turns[n])
+            stack_ref[h, blk, 0], stack_ref[h, blk, 1] = turn_h, turn_l
+            stack_ref[h, blk, 2] = writes[n].astype(BF16)
+            stack = stack_of(h, blk)
             key_t = key_of(h, blk).T
             changes.append(dot(jnp.concatenate([key_t, key_t], axis=1), stack))
             yield
         for n in range(count):
             step = eye_ref[...] - changes[n][:, :HEAD_DIM]
-            turn_ref[slot, n] = jnp.concatenate(split(step), axis=1)
+            turn_ref[slot, n, 0], turn_ref[slot, n, 1] = split(step)
             source_ref[slot, n] = changes[n][:, HEAD_DIM:]
             yield
 
@@ -450,27 +459,28 @@
             h, blk = place(it, n)
             i = n % 2
             high, low = split(states_now[i])
-            start_ref[h, blk] = high
-            both = turn_ref[slot, n]
+            start_ref[h, blk, 0] = high[:, :HEAD_DIM]
+            start_ref[h, blk, 1] = high[:, HEAD_DIM:]
+            turn_h, turn_l = turn_ref[slot, n, 0], turn_ref[slot, n, 1]
             moved = dot(
-                jnp.concatenate([both, both[:, :HEAD_DIM]], axis=1),
+                jnp.concatenate([turn_h, turn_l, turn_h], axis=1),
                 jnp.concatenate([high, high, low], axis=0),
             )
             states_now[i] = jnp.concatenate(
                 [moved[:, :HEAD_DIM], moved[:, HEAD_DIM:] + source_ref[slot, n]], axis=1
             )
+            if n >= count - 2:
+                x_ref[h] = states_now[i]
             yield
-        for i in range(2):
-            x_ref[2 * pair + i] = states_now[i]
-
-    def a_stream(it):
-        return 4 * count + BASE, solve(it)
-
-    def b_stream(it):
-        return 9 * count, transit(it)
-
-    def c_stream(it):
-        return count, compose(it)
+
+    def a_stream(it, first=0.0, last=1.0):
+        return 7 * count // 4 + BASE, solve(it), first, last
+
+    def b_stream(it, first=0.0, last=1.0):
+        return 9 * count, transit(it), first, last
+
+    def c_stream(it, first=0.0, last=1.0):
+        return count, compose(it), first, last
 
     def owner_of(pair, i):
         side = lax.rem(pair + core, 2)
@@ -501,7 +511,8 @@
     def post(pair):
         for i in range(2):
             h = 2 * pair + i
-            maps[h] = x_ref[h].astype(BF16)
+            maps[h, 0] = x_ref[h, :, :HEAD_DIM].astype(BF16)
+            maps[h, 1] = x_ref[h, :, HEAD_DIM:].astype(BF16)
 
             @pl.when((seq != owner_of(pair, i)) & (seq != peers - 1))
             def _():
@@ -523,10 +534,9 @@
                     def _():
                         send_map(pair, i, k).wait_recv()
 
-                    here = held[pair, k]
                     high, low = split(carry_ref[...])
-                    turn = here[:, :HEAD_DIM]
-                    state = here[:, HEAD_DIM:].astype(F32) + dot(
+                    turn = held[pair, k, 0]
+                    state = held[pair, k, 1].astype(F32) + dot(
                         jnp.concatenate([turn, turn], axis=1),
                         jnp.concatenate([high, low], axis=0),
                     )
@@ -581,8 +591,11 @@
         return 0
 
     lax.fori_loop(2, steps, step, 0)
-    weave(b_stream(steps - 1), c_stream(steps - 2))
-    weave(c_stream(steps - 1))
+    weave(
+        b_stream(steps - 1, 0.0, 9.0),
+        c_stream(steps - 2, 0.0, 6.0),
+        c_stream(steps - 1, 8.1, 9.1),
+    )
     post(pairs - 1)
     for h in range(heads):
         fetch_q(h).wait()
@@ -595,29 +608,49 @@
             for blk in range(blocks):
                 found = jnp.where(causal, dot_t(q_ref[h, blk], key_of(h, blk)), 0.0).astype(BF16)
                 scores.append(jnp.concatenate([found, found], axis=1))
-            drawn = [dot(score, stack_ref[h, blk]) for blk, score in enumerate(scores)]
+            drawn = [dot(score, stack_of(h, blk)) for blk, score in enumerate(scores)]
             for blk in range(blocks):
                 kept = (q_ref[h, blk].astype(F32) - drawn[blk][:, :HEAD_DIM]).astype(BF16)
-                out = dot(kept, start_ref[h, blk])
+                out = dot(kept, jnp.concatenate([start_ref[h, blk, 0], start_ref[h, blk, 1]], axis=1))
                 m_ref[h, blk] = out[:, :HEAD_DIM].astype(BF16)
                 o_ref[h, blk] = out[:, HEAD_DIM:] + drawn[blk][:, HEAD_DIM:]
 
-        @pl.when(pair != 1)
+        @pl.when(pair % 2 == 0)
         def _():
-            chain(jnp.maximum(pair, 1))
+            chain(1 + pair // 2)
 
         return 0
 
     lax.fori_loop(0, pairs, read, 0)
-    for pair in range(pairs):
+    for h in range(heads):
+        fetch_g(h).wait()
+
+    def wait_state(pair):
         for i in range(2):
 
             @pl.when((seq != owner_of(pair, i)) & (seq != 0))
             def _():
                 send_state(pair, i, seq).wait_recv()
 
-    for h in range(heads):
-        fetch_g(h).wait()
+    def blend(pair, t):
+        for i in range(2):
+            h = 2 * pair + i
+            query = q_ref[h, t].astype(F32)
+            unit = lax.rsqrt(jnp.sum(query * query, axis=1, keepdims=True) + 1e-06)
+            seen = unit * (o_ref[h, t] + dot(m_ref[h, t], s_ref[h]))
+            scale = lax.rsqrt(jnp.mean(seen * seen, axis=1, keepdims=True) + 1e-06)
+            gate = g_ref[h, t].astype(F32)
+            mixed[t, h] = (seen * scale * (gate / (1.0 + jnp.exp(-gate)))).astype(BF16)
+
+    def blend_pair(pair, _):
+        wait_state(pair)
+        for t in range(blocks):
+            blend(pair, t)
+        return 0
+
+    lax.fori_loop(0, pairs - 2, blend_pair, 0)
+    chain(pairs - 1)
+    blend_pair(pairs - 2, 0)
 
     def send(source, target, send_sem, recv_sem, t, device):
         return pltpu.make_async_remote_copy(
@@ -643,54 +676,62 @@
         cross_out[t] = (total[t] + far_in[t].astype(F32)).astype(BF16)
         cross(t).start()
 
-    def blend(t):
-        held_blocks = rows // span
-        for h in range(heads):
-            window = slice(t * held_blocks, (t + 1) * held_blocks)
-            query = q_ref[h, window].reshape(rows, HEAD_DIM).astype(F32)
-            unit = lax.rsqrt(jnp.sum(query * query, axis=1, keepdims=True) + 1e-06)
-            seen = o_ref[h, window].reshape(rows, HEAD_DIM) + dot(
-                m_ref[h, window].reshape(rows, HEAD_DIM), s_ref[h]
-            )
-            seen = unit * seen
-            scale = lax.rsqrt(jnp.mean(seen * seen, axis=1, keepdims=True) + 1e-06)
-            gate = g_ref[h, window].reshape(rows, HEAD_DIM).astype(F32)
-            mixed[t, :, h * HEAD_DIM : (h + 1) * HEAD_DIM] = (
-                seen * scale * (gate / (1.0 + jnp.exp(-gate)))
-            ).astype(BF16)
-
-    for t in range(PIECES):
-        blend(t)
-        if t == 0:
-            load(0).wait()
-        far_out[t] = dot(mixed[t], weight[0]).astype(BF16)
+    def rows_of(t, first, last):
+        return jnp.concatenate([mixed[t, h] for h in range(first, last)], axis=1)
+
+    def product(t, n):
+        return dot(rows_of(t, 0, heads), weight[n])
+
+    early = (heads - 2) * HEAD_DIM
+    load(0).wait()
+    total[0] = dot(rows_of(0, 0, heads - 2), weight[0, :early, :])
+    wait_state(pairs - 1)
+    blend(pairs - 1, 0)
+    far_out[0] = (total[0] + dot(rows_of(0, heads - 2, heads), weight[0, early:, :])).astype(BF16)
+    far(0).start()
+    load(1).wait()
+    total[0] = product(0, 1)
+
+    def first_half(t, _):
+        blend(pairs - 1, t)
+        far_out[t] = product(t, 0).astype(BF16)
         far(t).start()
-        if t == 0:
-            load(1).wait()
-        total[t] = dot(mixed[t], weight[1])
-        if t > 0:
-            pass_on(t - 1)
+        pass_on(t - 1)
+        total[t] = product(t, 1)
+        return 0
+
+    lax.fori_loop(1, blocks, first_half, 0)
     load(2).wait()
-    for t in range(PIECES):
-        near_out[t] = dot(mixed[t], weight[2]).astype(BF16)
+    near_out[0] = product(0, 2).astype(BF16)
+    near(0).start()
+    pass_on(blocks - 1)
+
+    def second_half(t, _):
+        near_out[t] = product(t, 2).astype(BF16)
         near(t).start()
-        if t == 0:
-            pass_on(PIECES - 1)
+        return 0
+
+    lax.fori_loop(1, blocks, second_half, 0)
     load(3).wait()
-    for t in range(PIECES):
-        total[t] = dot(mixed[t], weight[3])
+
+    def own_part(t, _):
+        total[t] = product(t, 3)
+        return 0
+
+    lax.fori_loop(0, blocks, own_part, 0)
 
     def put(t):
-        span_t = pl.ds(t * rows, rows)
-        return pltpu.make_async_copy(y_ref.at[span_t], y_hbm.at[span_t], y_sem.at[t])
-
-    for t in range(PIECES):
+        window = pl.ds(pl.multiple_of(t * span, span), span)
+        return pltpu.make_async_copy(y_ref.at[t], y_hbm.at[window], y_sem.at[t])
+
+    def close(t, _):
         near(t).wait()
         cross(t).wait()
-        y_ref[t * rows : (t + 1) * rows, :] = (
-            total[t] + near_in[t].astype(F32) + cross_in[t].astype(F32)
-        ).astype(BF16)
+        y_ref[t] = (total[t] + near_in[t].astype(F32) + cross_in[t].astype(F32)).astype(BF16)
         put(t).start()
+        return 0
+
+    lax.fori_loop(0, blocks, close, 0)
     for pair in range(pairs):
         for i in range(2):
 
@@ -706,7 +747,7 @@
                     def _():
                         send_state(pair, i, k).wait_send()
 
-    for t in range(PIECES):
+    for t in range(blocks):
         put(t).wait()
 
 
@@ -719,9 +760,10 @@
     batch = blocks // 2
     vmem = pl.BlockSpec(memory_space=pltpu.VMEM)
     hbm = pl.BlockSpec(memory_space=pl.ANY)
-    piece = (PIECES, tokens // PIECES, width)
+    piece = (blocks, SPAN, width)
     square = (HEAD_DIM, HEAD_DIM)
     wide = (HEAD_DIM, 2 * HEAD_DIM)
+    two = (2,) + square
     pairs = heads // 2
     dma = pltpu.SemaphoreType.DMA
     per_head = (heads, blocks, SPAN, HEAD_DIM)
@@ -737,40 +779,40 @@
             pltpu.VMEM(both, BF16),
             pltpu.VMEM(per_head, BF16),
             pltpu.VMEM((blocks, heads, 2 * SPAN), F32),
-            pltpu.VMEM((heads, blocks, 4 * SPAN, 2 * HEAD_DIM), BF16),
-            pltpu.VMEM((2, 2 * batch) + wide, BF16),
+            pltpu.VMEM((heads, blocks, 3) + square, BF16),
+            pltpu.VMEM((2, 2 * batch) + two, BF16),
             pltpu.VMEM((2, 2 * batch) + square, F32),
             pltpu.VMEM((heads,) + wide, F32),
-            pltpu.VMEM((heads, blocks) + wide, BF16),
-            pltpu.VMEM((2, 2 * batch) + wide, BF16),
+            pltpu.VMEM((heads, blocks) + two, BF16),
+            pltpu.VMEM((2, 2 * batch) + two, BF16),
             pltpu.VMEM((2, 2 * batch, BASE, 2 * SPAN), F32),
             pltpu.VMEM((2, 2, 2 * batch, 2 * SPAN), F32),
             pltpu.VMEM(square, F32),
-            pltpu.VMEM((heads,) + wide, BF16),
-            pltpu.VMEM((pairs, peers) + wide, BF16),
+            pltpu.VMEM((heads,) + two, BF16),
+            pltpu.VMEM((pairs, peers) + two, BF16),
             pltpu.VMEM(square, F32),
             pltpu.VMEM((pairs, peers) + square, BF16),
             pltpu.VMEM((heads,) + square, BF16),
             pltpu.VMEM(per_head, F32),
             pltpu.VMEM(per_head, BF16),
-            pltpu.VMEM((PIECES, tokens // PIECES, depth), BF16),
+            pltpu.VMEM((blocks, heads, SPAN, HEAD_DIM), BF16),
             pltpu.VMEM((4, depth, width), BF16),
             pltpu.VMEM(piece, F32),
         ]
         + [pltpu.VMEM(piece, BF16)] * 6
         + [
-            pltpu.VMEM((tokens, width), BF16),
+            pltpu.VMEM(piece, BF16),
             dma((2, heads)),
             dma((heads,)),
             dma((heads,)),
             dma((4,)),
-            dma((PIECES,)),
+            dma((blocks,)),
             dma((heads,)),
             dma((pairs, peers)),
             dma((pairs, peers)),
             dma((heads,)),
         ]
-        + [dma((PIECES,))] * 6,
+        + [dma((blocks,))] * 6,
         compiler_params=pltpu.CompilerParams(
             collective_id=0, has_side_effects=True, vmem_limit_bytes=VMEM_LIMIT
         ),

time: 61.6 us -> 63.4 us (1.029)
  Pallas kernels: 58.8 us -> 60.9 us
    pallas_call x1, Pallas kernels: 58.8 us -> 60.9 us  [fused(): pl.pallas_call(functools.partial(fused_kernel, seq_axis, peers, axis), in...]
where the time goes in v3:
time: 63.4 us; the launch traced here: 63.1 us
  Pallas kernels  60.9 us (96%)
  local copies, waits for them, and re-layouts  2.26 us (4%)
    pallas_call x1, Pallas kernels, fused(): pl.pallas_call(functools.partial(fused_kernel, seq_axis, peers, axis), in...  60.9 us
    unnamed x1, local copies, waits for them, and re-layouts  2.26 us

profile of v3, /device:TPU:24, one launch (start us, length us, event | category | flops | bytes accessed | tf_op | source)
XLA Modules:
  0.0 63.1 jit_solution(728318845655255682)
XLA Ops:
  0.0 60.9 %shard_map.64 = bf16[512,1024]{1,0:T(8,128)(2,1)} custom-call(bf16[8,64,1024]{2,1,0:T(8,128)(2,1)} %bitcast.6, bf16[2,8,64,1024]{3,2,1,0:T(8,128)(2,1)} %bitcast.4, bf16[2,8,64,1024]{3,2,1,0:T(8,128)(2,1)} %bitcast.5, f32[8,2,512]{2,1,0:T(2,128)} %b_ref.1, bf16[8,64,1024]{2,1,0:T(8,128)(2,1)} %bitcast.7, bf16[1024,4096]{1,0:T(8,128)(2,1)} %w_hbm.1), custom_call_target="tpu_custom_call" | custom-call | tf_op jit(solution)/shard_map/pallas_call | solution.py:771
  60.9 2.3 %copy.8 = bf16[512,1024]{1,0:T(8,128)(2,1)} copy(bf16[512,1024]{1,0:T(8,128)(2,1)} %shard_map.64) | data formatting | bytes 2097152

commit v4 on v3

--- a/solution.py
+++ b/solution.py
@@ -615,12 +615,9 @@
                 m_ref[h, blk] = out[:, :HEAD_DIM].astype(BF16)
                 o_ref[h, blk] = out[:, HEAD_DIM:] + drawn[blk][:, HEAD_DIM:]
 
-        @pl.when(pair % 2 == 0)
-        def _():
-            chain(1 + pair // 2)
-
         return 0
 
+    chain(1)
     lax.fori_loop(0, pairs, read, 0)
     for h in range(heads):
         fetch_g(h).wait()
@@ -642,15 +639,18 @@
             gate = g_ref[h, t].astype(F32)
             mixed[t, h] = (seen * scale * (gate / (1.0 + jnp.exp(-gate)))).astype(BF16)
 
-    def blend_pair(pair, _):
+    def blend_pair(pair):
         wait_state(pair)
-        for t in range(blocks):
-            blend(pair, t)
+        for blk in range(blocks):
+            blend(pair, blk)
+
+    def settle(pair, _):
+        chain(pair + 2)
+        blend_pair(pair)
         return 0
 
-    lax.fori_loop(0, pairs - 2, blend_pair, 0)
-    chain(pairs - 1)
-    blend_pair(pairs - 2, 0)
+    lax.fori_loop(0, pairs - 2, settle, 0)
+    blend_pair(pairs - 2)
 
     def send(source, target, send_sem, recv_sem, t, device):
         return pltpu.make_async_remote_copy(
@@ -676,62 +676,61 @@
         cross_out[t] = (total[t] + far_in[t].astype(F32)).astype(BF16)
         cross(t).start()
 
+    share = blocks // PIECES
+
     def rows_of(t, first, last):
-        return jnp.concatenate([mixed[t, h] for h in range(first, last)], axis=1)
+        return jnp.concatenate(
+            [
+                jnp.concatenate([mixed[t * share + b, h] for h in range(first, last)], axis=1)
+                for b in range(share)
+            ],
+            axis=0,
+        )
 
     def product(t, n):
         return dot(rows_of(t, 0, heads), weight[n])
+
+    def finish_piece(t):
+        for b in range(share):
+            blend(pairs - 1, t * share + b)
 
     early = (heads - 2) * HEAD_DIM
     load(0).wait()
     total[0] = dot(rows_of(0, 0, heads - 2), weight[0, :early, :])
     wait_state(pairs - 1)
-    blend(pairs - 1, 0)
+    finish_piece(0)
     far_out[0] = (total[0] + dot(rows_of(0, heads - 2, heads), weight[0, early:, :])).astype(BF16)
     far(0).start()
     load(1).wait()
     total[0] = product(0, 1)
-
-    def first_half(t, _):
-        blend(pairs - 1, t)
+    for t in range(1, PIECES):
+        finish_piece(t)
         far_out[t] = product(t, 0).astype(BF16)
         far(t).start()
+        if t > 1:
+            total[t] = product(t, 1)
         pass_on(t - 1)
-        total[t] = product(t, 1)
-        return 0
-
-    lax.fori_loop(1, blocks, first_half, 0)
+        if t == 1:
+            total[t] = product(t, 1)
     load(2).wait()
-    near_out[0] = product(0, 2).astype(BF16)
-    near(0).start()
-    pass_on(blocks - 1)
-
-    def second_half(t, _):
+    for t in range(PIECES):
         near_out[t] = product(t, 2).astype(BF16)
         near(t).start()
-        return 0
-
-    lax.fori_loop(1, blocks, second_half, 0)
+        if t == 0:
+            pass_on(PIECES - 1)
     load(3).wait()
-
-    def own_part(t, _):
+    for t in range(PIECES):
         total[t] = product(t, 3)
-        return 0
-
-    lax.fori_loop(0, blocks, own_part, 0)
 
     def put(t):
-        window = pl.ds(pl.multiple_of(t * span, span), span)
-        return pltpu.make_async_copy(y_ref.at[t], y_hbm.at[window], y_sem.at[t])
-
-    def close(t, _):
+        rows = y_ref.shape[1]
+        return pltpu.make_async_copy(y_ref.at[t], y_hbm.at[pl.ds(t * rows, rows)], y_sem.at[t])
+
+    for t in range(PIECES):
         near(t).wait()
         cross(t).wait()
         y_ref[t] = (total[t] + near_in[t].astype(F32) + cross_in[t].astype(F32)).astype(BF16)
         put(t).start()
-        return 0
-
-    lax.fori_loop(0, blocks, close, 0)
     for pair in range(pairs):
         for i in range(2):
 
@@ -747,7 +746,7 @@
                     def _():
                         send_state(pair, i, k).wait_send()
 
-    for t in range(blocks):
+    for t in range(PIECES):
         put(t).wait()
 
 
@@ -760,7 +759,7 @@
     batch = blocks // 2
     vmem = pl.BlockSpec(memory_space=pltpu.VMEM)
     hbm = pl.BlockSpec(memory_space=pl.ANY)
-    piece = (blocks, SPAN, width)
+    piece = (PIECES, tokens // PIECES, width)
     square = (HEAD_DIM, HEAD_DIM)
     wide = (HEAD_DIM, 2 * HEAD_DIM)
     two = (2,) + square
@@ -806,13 +805,13 @@
             dma((heads,)),
             dma((heads,)),
             dma((4,)),
-            dma((blocks,)),
+            dma((PIECES,)),
             dma((heads,)),
             dma((pairs, peers)),
             dma((pairs, peers)),
             dma((heads,)),
         ]
-        + [dma((blocks,))] * 6,
+        + [dma((PIECES,))] * 6,
         compiler_params=pltpu.CompilerParams(
             collective_id=0, has_side_effects=True, vmem_limit_bytes=VMEM_LIMIT
         ),

time: 63.4 us -> 62.1 us (0.979); the launches traced: 63.1 us -> 61.1 us
  Pallas kernels: 60.9 us -> 58.8 us
    pallas_call x1, Pallas kernels: 60.9 us -> 58.8 us  [fused(): pl.pallas_call(functools.partial(fused_kernel, seq_axis, peers, axis), in...]
where the time goes in v4:
time: 62.1 us; the launch traced here: 61.1 us
  Pallas kernels  58.8 us (95%)
  local copies, waits for them, and re-layouts  2.26 us (4%)
    pallas_call x1, Pallas kernels, fused(): pl.pallas_call(functools.partial(fused_kernel, seq_axis, peers, axis), in...  58.8 us
    unnamed x1, local copies, waits for them, and re-layouts  2.26 us

profile of v4, /device:TPU:24, one launch (start us, length us, event | category | flops | bytes accessed | tf_op | source)
XLA Modules:
  0.0 61.1 jit_solution(11659353786757010734)
XLA Ops:
  0.0 58.8 %shard_map.64 = bf16[512,1024]{1,0:T(8,128)(2,1)} custom-call(bf16[8,64,1024]{2,1,0:T(8,128)(2,1)} %bitcast.6, bf16[2,8,64,1024]{3,2,1,0:T(8,128)(2,1)} %bitcast.4, bf16[2,8,64,1024]{3,2,1,0:T(8,128)(2,1)} %bitcast.5, f32[8,2,512]{2,1,0:T(2,128)} %b_ref.1, bf16[8,64,1024]{2,1,0:T(8,128)(2,1)} %bitcast.7, bf16[1024,4096]{1,0:T(8,128)(2,1)} %w_hbm.1), custom_call_target="tpu_custom_call" | custom-call | tf_op jit(solution)/shard_map/pallas_call | solution.py:770
  58.8 2.3 %copy.8 = bf16[512,1024]{1,0:T(8,128)(2,1)} copy(bf16[512,1024]{1,0:T(8,128)(2,1)} %shard_map.64) | data formatting | bytes 2097152

commit v5 on v4

--- a/solution.py
+++ b/solution.py
@@ -188,6 +188,9 @@
                 state = maps[:, HEAD_DIM:].astype(F32) + dot(
                     jnp.concatenate([turn, turn], axis=1), jnp.concatenate([high, low], axis=0)
                 )
+
+
+FUSED_LIMIT = 52 * 1024 * 1024
 
 
 def dot_t(a, b):
@@ -298,12 +301,12 @@
 
 
 def fused_kernel(
-    seq_axis, peers, axis, q_hbm, k_hbm, v_hbm, b_ref, g_hbm, w_hbm, y_hbm,
-    q_ref, k_ref, v_ref, g_ref, beta_ref, stack_ref, turn_ref, source_ref, x_ref, start_ref,
+    seq_axis, peers, axis, q_hbm, k_hbm, v_hbm, b_hbm, g_hbm, w_hbm, y_ref,
+    b_ref, q_ref, k_ref, v_ref, g_ref, beta_ref, stack_ref, turn_ref, source_ref, x_ref, start_ref,
     low_ref, inv_ref, weight_ref, eye_ref,
     maps, held, carry_ref, states, s_ref, o_ref, m_ref,
-    mixed, weight, total, far_out, far_in, near_out, near_in, cross_out, cross_in, y_ref,
-    kv_sem, q_sem, g_sem, load_sem, y_sem, map_send, map_recv, back_send, back_recv,
+    mixed, weight, total, far_out, far_in, near_out, near_in, cross_out, cross_in,
+    b_sem, kv_sem, q_sem, g_sem, load_sem, map_send, map_recv, back_send, back_recv,
     far_send, far_recv, near_send, near_recv, cross_send, cross_recv,
 ):
     heads, blocks, span = q_ref.shape[0], q_ref.shape[1], q_ref.shape[2]
@@ -318,6 +321,37 @@
     beyond = 2 * (1 - chip) + 1 - core
     width = y_ref.shape[2]
 
+    def columns(h):
+        return pl.ds(pl.multiple_of(h * HEAD_DIM, HEAD_DIM), HEAD_DIM)
+
+    def fetch_kv(h):
+        return (
+            pltpu.make_async_copy(k_hbm.at[:, :, :, columns(h)], k_ref.at[h], kv_sem.at[0, h]),
+            pltpu.make_async_copy(v_hbm.at[:, :, :, columns(h)], v_ref.at[h], kv_sem.at[1, h]),
+        )
+
+    def fetch_q(h):
+        return pltpu.make_async_copy(q_hbm.at[:, :, columns(h)], q_ref.at[h], q_sem.at[h])
+
+    def fetch_g(h):
+        return pltpu.make_async_copy(g_hbm.at[:, :, columns(h)], g_ref.at[h], g_sem.at[h])
+
+    def load(n):
+        owner = (beyond, across, sibling, me)[n]
+        return pltpu.make_async_copy(
+            w_hbm.at[:, pl.ds(pl.multiple_of(owner * width, width), width)],
+            weight.at[n],
+            load_sem.at[n],
+        )
+
+    def start_kv(first, last):
+        for h in range(first, last):
+            for copy in fetch_kv(h):
+                copy.start()
+
+    fetch_b = pltpu.make_async_copy(b_hbm, b_ref, b_sem)
+    fetch_b.start()
+    start_kv(0, 2)
     barrier = pltpu.get_barrier_semaphore()
     for other in (sibling, across):
         pl.semaphore_signal(barrier, inc=1, device_id={axis: other}, device_id_type=MESH)
@@ -329,41 +363,14 @@
             device_id_type=MESH,
         )
 
-    def columns(h):
-        return pl.ds(pl.multiple_of(h * HEAD_DIM, HEAD_DIM), HEAD_DIM)
-
-    def fetch_kv(h):
-        return (
-            pltpu.make_async_copy(k_hbm.at[:, :, :, columns(h)], k_ref.at[h], kv_sem.at[0, h]),
-            pltpu.make_async_copy(v_hbm.at[:, :, :, columns(h)], v_ref.at[h], kv_sem.at[1, h]),
-        )
-
-    def fetch_q(h):
-        return pltpu.make_async_copy(q_hbm.at[:, :, columns(h)], q_ref.at[h], q_sem.at[h])
-
-    def fetch_g(h):
-        return pltpu.make_async_copy(g_hbm.at[:, :, columns(h)], g_ref.at[h], g_sem.at[h])
-
-    def load(n):
-        owner = (beyond, across, sibling, me)[n]
-        return pltpu.make_async_copy(
-            w_hbm.at[:, pl.ds(pl.multiple_of(owner * width, width), width)],
-            weight.at[n],
-            load_sem.at[n],
-        )
-
-    for h in range(heads):
-        for copy in fetch_kv(h):
-            copy.start()
-    for h in range(heads):
-        fetch_q(h).start()
-    for blk in range(blocks):
-        window = slice(blk * span, (blk + 1) * span)
-        beta_ref[blk] = jnp.concatenate([b_ref[:, 0, window], b_ref[:, 1, window]], axis=1)
     begin = (iota((HEAD_DIM, 2 * HEAD_DIM), 0) == iota((HEAD_DIM, 2 * HEAD_DIM), 1)).astype(F32)
     for h in range(heads):
         x_ref[h] = begin
     eye_ref[...] = (iota(eye_ref.shape, 0) == iota(eye_ref.shape, 1)).astype(F32)
+    fetch_b.wait()
+    for blk in range(blocks):
+        window = slice(blk * span, (blk + 1) * span)
+        beta_ref[blk] = jnp.concatenate([b_ref[:, 0, window], b_ref[:, 1, window]], axis=1)
 
     def place(it, n):
         pair, part = it // parts, it % parts
@@ -562,7 +569,10 @@
 
     steps = parts * pairs
     wait_kv(0)
+    start_kv(2, heads)
     weave(a_stream(0))
+    for h in range(heads):
+        fetch_q(h).start()
     for n in range(4):
         load(n).start()
     for h in range(heads):
@@ -722,15 +732,10 @@
     for t in range(PIECES):
         total[t] = product(t, 3)
 
-    def put(t):
-        rows = y_ref.shape[1]
-        return pltpu.make_async_copy(y_ref.at[t], y_hbm.at[pl.ds(t * rows, rows)], y_sem.at[t])
-
     for t in range(PIECES):
         near(t).wait()
         cross(t).wait()
         y_ref[t] = (total[t] + near_in[t].astype(F32) + cross_in[t].astype(F32)).astype(BF16)
-        put(t).start()
     for pair in range(pairs):
         for i in range(2):
 
@@ -745,9 +750,6 @@
                     @pl.when(seq != k)
                     def _():
                         send_state(pair, i, k).wait_send()
-
-    for t in range(PIECES):
-        put(t).wait()
 
 
 def fused(queries, keys, values, betas, gate, out_weight, seq_axis, axis):
@@ -757,8 +759,7 @@
     width = out_weight.shape[1] // lax.axis_size(axis)
     blocks = tokens // SPAN
     batch = blocks // 2
-    vmem = pl.BlockSpec(memory_space=pltpu.VMEM)
-    hbm = pl.BlockSpec(memory_space=pl.ANY)
+    hbm = pl.BlockSpec(memory_space=pltpu.HBM)
     piece = (PIECES, tokens // PIECES, width)
     square = (HEAD_DIM, HEAD_DIM)
     wide = (HEAD_DIM, 2 * HEAD_DIM)
@@ -769,10 +770,11 @@
     both = (heads, 2, blocks, SPAN, HEAD_DIM)
     return pl.pallas_call(
         functools.partial(fused_kernel, seq_axis, peers, axis),
-        in_specs=[hbm, hbm, hbm, vmem, hbm, hbm],
-        out_specs=hbm,
-        out_shape=jax.ShapeDtypeStruct((tokens, width), BF16),
+        in_specs=[hbm] * 6,
+        out_specs=pl.BlockSpec(memory_space=pltpu.VMEM),
+        out_shape=jax.ShapeDtypeStruct((PIECES, tokens // PIECES, width), BF16),
         scratch_shapes=[
+            pltpu.VMEM(betas.shape, F32),
             pltpu.VMEM(per_head, BF16),
             pltpu.VMEM(both, BF16),
             pltpu.VMEM(both, BF16),
@@ -800,12 +802,11 @@
         ]
         + [pltpu.VMEM(piece, BF16)] * 6
         + [
-            pltpu.VMEM(piece, BF16),
+            dma,
             dma((2, heads)),
             dma((heads,)),
             dma((heads,)),
             dma((4,)),
-            dma((PIECES,)),
             dma((heads,)),
             dma((pairs, peers)),
             dma((pairs, peers)),
@@ -813,7 +814,7 @@
         ]
         + [dma((PIECES,))] * 6,
         compiler_params=pltpu.CompilerParams(
-            collective_id=0, has_side_effects=True, vmem_limit_bytes=VMEM_LIMIT
+            collective_id=0, has_side_effects=True, vmem_limit_bytes=FUSED_LIMIT
         ),
     )(
         queries.reshape(blocks, SPAN, depth),
@@ -822,7 +823,7 @@
         betas,
         gate.reshape(blocks, SPAN, depth),
         out_weight,
-    )
+    ).reshape(tokens, width)
 
 
 def start_state(maps, axis):

time: 62.1 us -> 60.2 us (0.969)
  Pallas kernels: 58.8 us -> 57.4 us
    pallas_call x1, Pallas kernels: 58.8 us -> 57.4 us  [fused(): pl.pallas_call(functools.partial(fused_kernel, seq_axis, peers, axis), in...]
    unnamed x1 -> x3, local copies, waits for them, and re-layouts: 2.26 us -> 1.73 us
where the time goes in v5:
time: 60.2 us; the launch traced here: 59.2 us
  Pallas kernels  57.4 us (95%)
  local copies, waits for them, and re-layouts  1.73 us (3%)
    pallas_call x1, Pallas kernels, fused(): pl.pallas_call(functools.partial(fused_kernel, seq_axis, peers, axis), in...  57.4 us
    unnamed x3, local copies, waits for them, and re-layouts  1.73 us

profile of v5, /device:TPU:24, one launch (start us, length us, event | category | flops | bytes accessed | tf_op | source)
XLA Modules:
  0.0 59.2 jit_solution(10088106087231349288)
XLA Ops:
  0.0 0.0 copy-start
  0.0 0.8 %copy-done = f32[8,2,512]{2,1,0:T(2,128)S(1)} copy-done((f32[8,2,512]{2,1,0:T(2,128)S(1)}, f32[8,2,512]{2,1,0:T(2,128)}, u32[]{:S(2)}) %copy-start) | copy-done | bytes 32792
  0.8 57.4 %shard_map.64 = bf16[4,128,1024]{2,1,0:T(8,128)(2,1)S(1)} custom-call(bf16[8,64,1024]{2,1,0:T(8,128)(2,1)} %bitcast.8, bf16[2,8,64,1024]{3,2,1,0:T(8,128)(2,1)} %bitcast.6, bf16[2,8,64,1024]{3,2,1,0:T(8,128)(2,1)} %bitcast.7, f32[8,2,512]{2,1,0:T(2,128)S(1)} %copy-done, bf16[8,64,1024]{2,1,0:T(8,128)(2,1)} %bitcast.9, bf16[1024,4096]{1,0:T(8,128)(2,1)} %w_hbm.1), custom_call_target="tpu_custom_call" | custom-call | tf_op jit(solution)/shard_map/pallas_call | solution.py:771
  58.2 1.0 %copy.8 = bf16[512,1024]{1,0:T(8,128)(2,1)} copy(bf16[512,1024]{1,0:T(8,128)(2,1)S(1)} %bitcast.5) | data formatting | bytes 2097152
Async XLA Ops:
  0.0 0.8 %copy-start = (f32[8,2,512]{2,1,0:T(2,128)S(1)}, f32[8,2,512]{2,1,0:T(2,128)}, u32[]{:S(2)}) copy-start(f32[8,2,512]{2,1,0:T(2,128)} %b_hbm.1) | copy-start | bytes 98308

commit v6 on v5

--- a/solution.py
+++ b/solution.py
@@ -373,7 +373,7 @@
         beta_ref[blk] = jnp.concatenate([b_ref[:, 0, window], b_ref[:, 1, window]], axis=1)
 
     def place(it, n):
-        pair, part = it // parts, it % parts
+        pair, part = it
         return 2 * pair + n % 2, part * batch + n // 2
 
     count = 2 * batch
@@ -392,7 +392,7 @@
         )
 
     def solve(it):
-        slot = it % 2
+        slot = it[1]
         grams, squares = [], []
         for n in range(count):
             key = key_of(*place(it, n))
@@ -425,7 +425,7 @@
             inv_ref[slot, n] = inv[n]
 
     def transit(it):
-        slot = it % 2
+        slot = it[1]
 
         def pieces(n):
             return low_ref[slot, n, 0], low_ref[slot, n, 1]
@@ -459,8 +459,8 @@
             yield
 
     def compose(it):
-        slot = it % 2
-        pair, part = it // parts, it % parts
+        slot = it[1]
+        pair, _ = it
         states_now = [x_ref[2 * pair + i] for i in range(2)]
         for n in range(count):
             h, blk = place(it, n)
@@ -481,7 +481,7 @@
             yield
 
     def a_stream(it, first=0.0, last=1.0):
-        return 7 * count // 4 + BASE, solve(it), first, last
+        return 7 * count // 4 + BASE + 1, solve(it), first, last
 
     def b_stream(it, first=0.0, last=1.0):
         return 9 * count, transit(it), first, last
@@ -567,44 +567,44 @@
             for copy in fetch_kv(2 * pair + i):
                 copy.wait()
 
-    steps = parts * pairs
     wait_kv(0)
     start_kv(2, heads)
-    weave(a_stream(0))
     for h in range(heads):
         fetch_q(h).start()
     for n in range(4):
         load(n).start()
     for h in range(heads):
         fetch_g(h).start()
-    weave(a_stream(1), b_stream(0))
-
-    def step(it, _):
-        @pl.when(it % parts == 0)
-        def _():
-            wait_kv(it // parts)
-
-        weave(a_stream(it), b_stream(it - 1), c_stream(it - 2))
-
-        @pl.when(it == parts + 1)
+    weave(
+        a_stream((0, 0), 0.0, 1.0),
+        a_stream((0, 1), 0.5, 2.0),
+        b_stream((0, 0), 1.1, 2.1),
+    )
+
+    def step(pair, _):
+        wait_kv(pair)
+        weave(
+            a_stream((pair, 0), 0.0, 1.0),
+            b_stream((pair - 1, 1), 0.0, 1.0),
+            c_stream((pair - 1, 0), 0.0, 1.0),
+            a_stream((pair, 1), 1.05, 2.0),
+            b_stream((pair, 0), 1.05, 2.0),
+            c_stream((pair - 1, 1), 1.05, 2.0),
+        )
+
+        @pl.when(pair == 1)
         def _():
             pl.semaphore_wait(barrier, peers + 1)
 
-        @pl.when(it % parts == 1)
-        def _():
-            post(it // parts - 1)
-
-        @pl.when(it == steps - 2)
-        def _():
-            chain(0)
-
+        post(pair - 1)
         return 0
 
-    lax.fori_loop(2, steps, step, 0)
+    lax.fori_loop(1, pairs, step, 0)
+    chain(0)
     weave(
-        b_stream(steps - 1, 0.0, 9.0),
-        c_stream(steps - 2, 0.0, 6.0),
-        c_stream(steps - 1, 8.1, 9.1),
+        b_stream((pairs - 1, 1), 0.0, 9.0),
+        c_stream((pairs - 1, 0), 0.0, 6.0),
+        c_stream((pairs - 1, 1), 8.1, 9.1),
     )
     post(pairs - 1)
     for h in range(heads):
@@ -772,7 +772,7 @@
         functools.partial(fused_kernel, seq_axis, peers, axis),
         in_specs=[hbm] * 6,
         out_specs=pl.BlockSpec(memory_space=pltpu.VMEM),
-        out_shape=jax.ShapeDtypeStruct((PIECES, tokens // PIECES, width), BF16),
+        out_shape=jax.ShapeDtypeStruct(piece, BF16),
         scratch_shapes=[
             pltpu.VMEM(betas.shape, F32),
             pltpu.VMEM(per_head, BF16),

time: 60.2 us -> 58.5 us (0.972)
  Pallas kernels: 57.4 us -> 55.7 us
    pallas_call x1, Pallas kernels: 57.4 us -> 55.7 us  [fused(): pl.pallas_call(functools.partial(fused_kernel, seq_axis, peers, axis), in...]
where the time goes in v6:
time: 58.5 us; the launch traced here: 57.4 us
  Pallas kernels  55.7 us (95%)
  local copies, waits for them, and re-layouts  1.73 us (3%)
    pallas_call x1, Pallas kernels, fused(): pl.pallas_call(functools.partial(fused_kernel, seq_axis, peers, axis), in...  55.7 us
    unnamed x3, local copies, waits for them, and re-layouts  1.73 us

profile of v6, /device:TPU:24, one launch (start us, length us, event | category | flops | bytes accessed | tf_op | source)
XLA Modules:
  0.0 57.4 jit_solution(16824068477464002798)
XLA Ops:
  0.0 0.0 copy-start
  0.0 0.8 %copy-done = f32[8,2,512]{2,1,0:T(2,128)S(1)} copy-done((f32[8,2,512]{2,1,0:T(2,128)S(1)}, f32[8,2,512]{2,1,0:T(2,128)}, u32[]{:S(2)}) %copy-start) | copy-done | bytes 32792
  0.8 55.7 %shard_map.64 = bf16[4,128,1024]{2,1,0:T(8,128)(2,1)S(1)} custom-call(bf16[8,64,1024]{2,1,0:T(8,128)(2,1)} %bitcast.8, bf16[2,8,64,1024]{3,2,1,0:T(8,128)(2,1)} %bitcast.6, bf16[2,8,64,1024]{3,2,1,0:T(8,128)(2,1)} %bitcast.7, f32[8,2,512]{2,1,0:T(2,128)S(1)} %copy-done, bf16[8,64,1024]{2,1,0:T(8,128)(2,1)} %bitcast.9, bf16[1024,4096]{1,0:T(8,128)(2,1)} %w_hbm.1), custom_call_target="tpu_custom_call" | custom-call | tf_op jit(solution)/shard_map/pallas_call | solution.py:771
  56.5 1.0 %copy.8 = bf16[512,1024]{1,0:T(8,128)(2,1)} copy(bf16[512,1024]{1,0:T(8,128)(2,1)S(1)} %bitcast.5) | data formatting | bytes 2097152
Async XLA Ops:
  0.0 0.8 %copy-start = (f32[8,2,512]{2,1,0:T(2,128)S(1)}, f32[8,2,512]{2,1,0:T(2,128)}, u32[]{:S(2)}) copy-start(f32[8,2,512]{2,1,0:T(2,128)} %b_hbm.1) | copy-start | bytes 98308

commit v7 on v6

--- a/solution.py
+++ b/solution.py
@@ -345,9 +345,9 @@
         )
 
     def start_kv(first, last):
-        for h in range(first, last):
-            for copy in fetch_kv(h):
-                copy.start()
+        for n in range(2):
+            for h in range(first, last):
+                fetch_kv(h)[n].start()
 
     fetch_b = pltpu.make_async_copy(b_hbm, b_ref, b_sem)
     fetch_b.start()
@@ -363,9 +363,6 @@
             device_id_type=MESH,
         )
 
-    begin = (iota((HEAD_DIM, 2 * HEAD_DIM), 0) == iota((HEAD_DIM, 2 * HEAD_DIM), 1)).astype(F32)
-    for h in range(heads):
-        x_ref[h] = begin
     eye_ref[...] = (iota(eye_ref.shape, 0) == iota(eye_ref.shape, 1)).astype(F32)
     fetch_b.wait()
     for blk in range(blocks):
@@ -461,10 +458,17 @@
     def compose(it):
         slot = it[1]
         pair, _ = it
-        states_now = [x_ref[2 * pair + i] for i in range(2)]
+        states_now = [None if it[1] == 0 else x_ref[2 * pair + i] for i in range(2)]
         for n in range(count):
             h, blk = place(it, n)
             i = n % 2
+            if blk == 0:
+                turn_h, turn_l = turn_ref[slot, n, 0], turn_ref[slot, n, 1]
+                states_now[i] = jnp.concatenate(
+                    [turn_h.astype(F32) + turn_l.astype(F32), source_ref[slot, n]], axis=1
+                )
+                yield
+                continue
             high, low = split(states_now[i])
             start_ref[h, blk, 0] = high[:, :HEAD_DIM]
             start_ref[h, blk, 1] = high[:, HEAD_DIM:]
@@ -567,7 +571,13 @@
             for copy in fetch_kv(2 * pair + i):
                 copy.wait()
 
-    wait_kv(0)
+    def after_values(pair, stream):
+        for i in range(2):
+            fetch_kv(2 * pair + i)[1].wait()
+        yield from stream
+
+    for h in range(2):
+        fetch_kv(h)[0].wait()
     start_kv(2, heads)
     for h in range(heads):
         fetch_q(h).start()
@@ -578,7 +588,7 @@
     weave(
         a_stream((0, 0), 0.0, 1.0),
         a_stream((0, 1), 0.5, 2.0),
-        b_stream((0, 0), 1.1, 2.1),
+        (9 * count, after_values(0, transit((0, 0))), 1.1, 2.1),
     )
 
     def step(pair, _):
@@ -621,6 +631,10 @@
             drawn = [dot(score, stack_of(h, blk)) for blk, score in enumerate(scores)]
             for blk in range(blocks):
                 kept = (q_ref[h, blk].astype(F32) - drawn[blk][:, :HEAD_DIM]).astype(BF16)
+                if blk == 0:
+                    m_ref[h, blk] = kept
+                    o_ref[h, blk] = drawn[blk][:, HEAD_DIM:]
+                    continue
                 out = dot(kept, jnp.concatenate([start_ref[h, blk, 0], start_ref[h, blk, 1]], axis=1))
                 m_ref[h, blk] = out[:, :HEAD_DIM].astype(BF16)
                 o_ref[h, blk] = out[:, HEAD_DIM:] + drawn[blk][:, HEAD_DIM:]
@@ -655,12 +669,15 @@
             blend(pair, blk)
 
     def settle(pair, _):
-        chain(pair + 2)
         blend_pair(pair)
         return 0
 
-    lax.fori_loop(0, pairs - 2, settle, 0)
-    blend_pair(pairs - 2)
+    def link(pair, _):
+        chain(pair)
+        return 0
+
+    lax.fori_loop(2, pairs, link, 0)
+    lax.fori_loop(0, pairs - 1, settle, 0)
 
     def send(source, target, send_sem, recv_sem, t, device):
         return pltpu.make_async_remote_copy(
@@ -820,7 +837,7 @@
         queries.reshape(blocks, SPAN, depth),
         keys.reshape(2, blocks, SPAN, depth),
         values.reshape(2, blocks, SPAN, depth),
-        betas,
+        pltpu.with_memory_space_constraint(betas, pltpu.HBM),
         gate.reshape(blocks, SPAN, depth),
         out_weight,
     ).reshape(tokens, width)

time: 58.5 us -> 57.7 us (0.986); the launches traced: 57.4 us -> 57.6 us
  Pallas kernels: 55.7 us -> 56.6 us
  local copies, waits for them, and re-layouts: 1.73 us -> 0.97 us
    pallas_call x1, Pallas kernels: 55.7 us -> 56.6 us  [fused(): pl.pallas_call(functools.partial(fused_kernel, seq_axis, peers, axis), in...]
    unnamed x3 -> x1, local copies, waits for them, and re-layouts: 1.73 us -> 0.97 us
where the time goes in v7:
time: 57.7 us; the launch traced here: 57.6 us
  Pallas kernels  56.6 us (98%)
  local copies, waits for them, and re-layouts  0.97 us (2%)
    pallas_call x1, Pallas kernels, fused(): pl.pallas_call(functools.partial(fused_kernel, seq_axis, peers, axis), in...  56.6 us

profile of v7, /device:TPU:24, one launch (start us, length us, event | category | flops | bytes accessed | tf_op | source)
XLA Modules:
  0.0 57.6 jit_solution(12496246188546599911)
XLA Ops:
  0.0 56.6 %shard_map.64 = bf16[4,128,1024]{2,1,0:T(8,128)(2,1)S(1)} custom-call(bf16[8,64,1024]{2,1,0:T(8,128)(2,1)} %bitcast.8, bf16[2,8,64,1024]{3,2,1,0:T(8,128)(2,1)} %bitcast.6, bf16[2,8,64,1024]{3,2,1,0:T(8,128)(2,1)} %bitcast.7, f32[8,2,512]{2,1,0:T(2,128)} %b_hbm.1, bf16[8,64,1024]{2,1,0:T(8,128)(2,1)} %bitcast.9, bf16[1024,4096]{1,0:T(8,128)(2,1)} %w_hbm.1), custom_call_target="tpu_custom_call" | custom-call | tf_op jit(solution)/shard_map/pallas_call | solution.py:788
  56.6 1.0 %copy.8 = bf16[512,1024]{1,0:T(8,128)(2,1)} copy(bf16[512,1024]{1,0:T(8,128)(2,1)S(1)} %bitcast.5) | data formatting | bytes 2097152

commit v8 on v7

--- a/solution.py
+++ b/solution.py
@@ -319,7 +319,7 @@
     sibling = 2 * chip + 1 - core
     across = 2 * (1 - chip) + core
     beyond = 2 * (1 - chip) + 1 - core
-    width = y_ref.shape[2]
+    width = y_ref.shape[1]
 
     def columns(h):
         return pl.ds(pl.multiple_of(h * HEAD_DIM, HEAD_DIM), HEAD_DIM)
@@ -610,7 +610,6 @@
         return 0
 
     lax.fori_loop(1, pairs, step, 0)
-    chain(0)
     weave(
         b_stream((pairs - 1, 1), 0.0, 9.0),
         c_stream((pairs - 1, 0), 0.0, 6.0),
@@ -641,7 +640,11 @@
 
         return 0
 
-    chain(1)
+    def link(pair, _):
+        chain(pair)
+        return 0
+
+    lax.fori_loop(0, 2, link, 0)
     lax.fori_loop(0, pairs, read, 0)
     for h in range(heads):
         fetch_g(h).wait()
@@ -672,17 +675,19 @@
         blend_pair(pair)
         return 0
 
-    def link(pair, _):
-        chain(pair)
-        return 0
-
     lax.fori_loop(2, pairs, link, 0)
     lax.fori_loop(0, pairs - 1, settle, 0)
 
+    sizes = [1, 1] + [2] * ((blocks - 4) // 2) + [1, 1]
+    starts = [sum(sizes[:t]) for t in range(len(sizes))]
+
+    def rows(t):
+        return pl.ds(starts[t] * span, sizes[t] * span)
+
     def send(source, target, send_sem, recv_sem, t, device):
         return pltpu.make_async_remote_copy(
-            src_ref=source.at[t],
-            dst_ref=target.at[t],
+            src_ref=source.at[rows(t)],
+            dst_ref=target.at[rows(t)],
             send_sem=send_sem.at[t],
             recv_sem=recv_sem.at[t],
             device_id={axis: device},
@@ -700,59 +705,59 @@
 
     def pass_on(t):
         far(t).wait()
-        cross_out[t] = (total[t] + far_in[t].astype(F32)).astype(BF16)
+        cross_out[rows(t)] = (total[rows(t)] + far_in[rows(t)].astype(F32)).astype(BF16)
         cross(t).start()
 
-    share = blocks // PIECES
-
-    def rows_of(t, first, last):
+    def mixed_of(t, first, last):
         return jnp.concatenate(
             [
-                jnp.concatenate([mixed[t * share + b, h] for h in range(first, last)], axis=1)
-                for b in range(share)
+                jnp.concatenate([mixed[starts[t] + b, h] for h in range(first, last)], axis=1)
+                for b in range(sizes[t])
             ],
             axis=0,
         )
 
     def product(t, n):
-        return dot(rows_of(t, 0, heads), weight[n])
+        return dot(mixed_of(t, 0, heads), weight[n])
 
     def finish_piece(t):
-        for b in range(share):
-            blend(pairs - 1, t * share + b)
-
+        for b in range(sizes[t]):
+            blend(pairs - 1, starts[t] + b)
+
+    count_pieces = len(sizes)
     early = (heads - 2) * HEAD_DIM
     load(0).wait()
-    total[0] = dot(rows_of(0, 0, heads - 2), weight[0, :early, :])
+    total[rows(0)] = dot(mixed_of(0, 0, heads - 2), weight[0, :early, :])
     wait_state(pairs - 1)
     finish_piece(0)
-    far_out[0] = (total[0] + dot(rows_of(0, heads - 2, heads), weight[0, early:, :])).astype(BF16)
+    late = dot(mixed_of(0, heads - 2, heads), weight[0, early:, :])
+    far_out[rows(0)] = (total[rows(0)] + late).astype(BF16)
     far(0).start()
     load(1).wait()
-    total[0] = product(0, 1)
-    for t in range(1, PIECES):
-        finish_piece(t)
-        far_out[t] = product(t, 0).astype(BF16)
+    finish_piece(1)
+    total[rows(0)] = product(0, 1)
+    for t in range(1, count_pieces):
+        if t > 1:
+            finish_piece(t)
+        far_out[rows(t)] = product(t, 0).astype(BF16)
         far(t).start()
-        if t > 1:
-            total[t] = product(t, 1)
         pass_on(t - 1)
-        if t == 1:
-            total[t] = product(t, 1)
+        total[rows(t)] = product(t, 1)
     load(2).wait()
-    for t in range(PIECES):
-        near_out[t] = product(t, 2).astype(BF16)
+    for t in range(count_pieces):
+        near_out[rows(t)] = product(t, 2).astype(BF16)
         near(t).start()
         if t == 0:
-            pass_on(PIECES - 1)
+            pass_on(count_pieces - 1)
     load(3).wait()
-    for t in range(PIECES):
-        total[t] = product(t, 3)
-
-    for t in range(PIECES):
+    for t in range(count_pieces):
+        total[rows(t)] = product(t, 3)
+    for t in range(count_pieces):
         near(t).wait()
+        total[rows(t)] = total[rows(t)] + near_in[rows(t)].astype(F32)
+    for t in range(count_pieces):
         cross(t).wait()
-        y_ref[t] = (total[t] + near_in[t].astype(F32) + cross_in[t].astype(F32)).astype(BF16)
+        y_ref[rows(t)] = (total[rows(t)] + cross_in[rows(t)].astype(F32)).astype(BF16)
     for pair in range(pairs):
         for i in range(2):
 
@@ -777,7 +782,8 @@
     blocks = tokens // SPAN
     batch = blocks // 2
     hbm = pl.BlockSpec(memory_space=pltpu.HBM)
-    piece = (PIECES, tokens // PIECES, width)
+    piece = (tokens, width)
+    pieces = blocks // 2 + 2
     square = (HEAD_DIM, HEAD_DIM)
     wide = (HEAD_DIM, 2 * HEAD_DIM)
     two = (2,) + square
@@ -829,7 +835,7 @@
             dma((pairs, peers)),
             dma((heads,)),
         ]
-        + [dma((PIECES,))] * 6,
+        + [dma((pieces,))] * 6,
         compiler_params=pltpu.CompilerParams(
             collective_id=0, has_side_effects=True, vmem_limit_bytes=FUSED_LIMIT
         ),
@@ -840,7 +846,7 @@
         pltpu.with_memory_space_constraint(betas, pltpu.HBM),
         gate.reshape(blocks, SPAN, depth),
         out_weight,
-    ).reshape(tokens, width)
+    )
 
 
 def start_state(maps, axis):

time: 57.7 us -> 57.6 us (level)
  no operation moved by 1% of the time
where the time goes in v8:
time: 57.6 us; the launch traced here: 57.4 us
  Pallas kernels  56.4 us (98%)
  local copies, waits for them, and re-layouts  0.97 us (2%)
    pallas_call x1, Pallas kernels, fused(): pl.pallas_call(functools.partial(fused_kernel, seq_axis, peers, axis), in...  56.4 us

profile of v8, /device:TPU:24, one launch (start us, length us, event | category | flops | bytes accessed | tf_op | source)
XLA Modules:
  0.0 57.4 jit_solution(5968088624384884338)
XLA Ops:
  0.0 56.4 %shard_map.64 = bf16[512,1024]{1,0:T(8,128)(2,1)S(1)} custom-call(bf16[8,64,1024]{2,1,0:T(8,128)(2,1)} %bitcast.6, bf16[2,8,64,1024]{3,2,1,0:T(8,128)(2,1)} %bitcast.4, bf16[2,8,64,1024]{3,2,1,0:T(8,128)(2,1)} %bitcast.5, f32[8,2,512]{2,1,0:T(2,128)} %b_hbm.1, bf16[8,64,1024]{2,1,0:T(8,128)(2,1)} %bitcast.7, bf16[1024,4096]{1,0:T(8,128)(2,1)} %w_hbm.1), custom_call_target="tpu_custom_call" | custom-call | tf_op jit(solution)/shard_map/pallas_call | solution.py:794
  56.4 1.0 %copy.8 = bf16[512,1024]{1,0:T(8,128)(2,1)} copy(bf16[512,1024]{1,0:T(8,128)(2,1)S(1)} %shard_map.64) | data formatting | bytes 2097152

commit v9 on v8

--- a/solution.py
+++ b/solution.py
@@ -587,8 +587,8 @@
         fetch_g(h).start()
     weave(
         a_stream((0, 0), 0.0, 1.0),
-        a_stream((0, 1), 0.5, 2.0),
-        (9 * count, after_values(0, transit((0, 0))), 1.1, 2.1),
+        a_stream((0, 1), 0.8, 2.0),
+        (9 * count, after_values(0, transit((0, 0))), 1.0, 2.1),
     )
 
     def step(pair, _):
@@ -645,7 +645,9 @@
         return 0
 
     lax.fori_loop(0, 2, link, 0)
-    lax.fori_loop(0, pairs, read, 0)
+    lax.fori_loop(0, pairs - 1, read, 0)
+    lax.fori_loop(2, pairs, link, 0)
+    read(pairs - 1, 0)
     for h in range(heads):
         fetch_g(h).wait()
 
@@ -675,7 +677,6 @@
         blend_pair(pair)
         return 0
 
-    lax.fori_loop(2, pairs, link, 0)
     lax.fori_loop(0, pairs - 1, settle, 0)
 
     sizes = [1, 1] + [2] * ((blocks - 4) // 2) + [1, 1]

time: 57.6 us -> 56.1 us (0.974)
  Pallas kernels: 56.4 us -> 54.9 us
    pallas_call x1, Pallas kernels: 56.4 us -> 54.9 us  [fused(): pl.pallas_call(functools.partial(fused_kernel, seq_axis, peers, axis), in...]
where the time goes in v9:
time: 56.1 us; the launch traced here: 55.9 us
  Pallas kernels  54.9 us (98%)
  local copies, waits for them, and re-layouts  0.97 us (2%)
    pallas_call x1, Pallas kernels, fused(): pl.pallas_call(functools.partial(fused_kernel, seq_axis, peers, axis), in...  54.9 us

profile of v9, /device:TPU:24, one launch (start us, length us, event | category | flops | bytes accessed | tf_op | source)
XLA Modules:
  0.0 55.9 jit_solution(15216310067196142604)
XLA Ops:
  0.0 54.9 %shard_map.64 = bf16[512,1024]{1,0:T(8,128)(2,1)S(1)} custom-call(bf16[8,64,1024]{2,1,0:T(8,128)(2,1)} %bitcast.6, bf16[2,8,64,1024]{3,2,1,0:T(8,128)(2,1)} %bitcast.4, bf16[2,8,64,1024]{3,2,1,0:T(8,128)(2,1)} %bitcast.5, f32[8,2,512]{2,1,0:T(2,128)} %b_hbm.1, bf16[8,64,1024]{2,1,0:T(8,128)(2,1)} %bitcast.7, bf16[1024,4096]{1,0:T(8,128)(2,1)} %w_hbm.1), custom_call_target="tpu_custom_call" | custom-call | tf_op jit(solution)/shard_map/pallas_call | solution.py:795
  54.9 1.0 %copy.8 = bf16[512,1024]{1,0:T(8,128)(2,1)} copy(bf16[512,1024]{1,0:T(8,128)(2,1)S(1)} %shard_map.64) | data formatting | bytes 2097152

commit v10 on v9

--- a/solution.py
+++ b/solution.py
@@ -645,9 +645,9 @@
         return 0
 
     lax.fori_loop(0, 2, link, 0)
-    lax.fori_loop(0, pairs - 1, read, 0)
+    lax.fori_loop(0, pairs // 2, read, 0)
     lax.fori_loop(2, pairs, link, 0)
-    read(pairs - 1, 0)
+    lax.fori_loop(pairs // 2, pairs, read, 0)
     for h in range(heads):
         fetch_g(h).wait()
 

time: 56.1 us -> 56.1 us (level)
  no operation moved by 1% of the time
where the time goes in v10:
time: 56.1 us; the launch traced here: 55.9 us
  Pallas kernels  54.9 us (98%)
  local copies, waits for them, and re-layouts  0.97 us (2%)
    pallas_call x1, Pallas kernels, fused(): pl.pallas_call(functools.partial(fused_kernel, seq_axis, peers, axis), in...  54.9 us

profile of v10, /device:TPU:24, one launch (start us, length us, event | category | flops | bytes accessed | tf_op | source)
XLA Modules:
  0.0 55.9 jit_solution(682073320618794980)
XLA Ops:
  0.0 54.9 %shard_map.64 = bf16[512,1024]{1,0:T(8,128)(2,1)S(1)} custom-call(bf16[8,64,1024]{2,1,0:T(8,128)(2,1)} %bitcast.6, bf16[2,8,64,1024]{3,2,1,0:T(8,128)(2,1)} %bitcast.4, bf16[2,8,64,1024]{3,2,1,0:T(8,128)(2,1)} %bitcast.5, f32[8,2,512]{2,1,0:T(2,128)} %b_hbm.1, bf16[8,64,1024]{2,1,0:T(8,128)(2,1)} %bitcast.7, bf16[1024,4096]{1,0:T(8,128)(2,1)} %w_hbm.1), custom_call_target="tpu_custom_call" | custom-call | tf_op jit(solution)/shard_map/pallas_call | solution.py:795
  54.9 1.0 %copy.8 = bf16[512,1024]{1,0:T(8,128)(2,1)} copy(bf16[512,1024]{1,0:T(8,128)(2,1)S(1)} %shard_map.64) | data formatting | bytes 2097152

commit v11 on v10

--- a/solution.py
+++ b/solution.py
@@ -503,7 +503,7 @@
             src_ref=maps.at[h],
             dst_ref=held.at[pair, source],
             send_sem=map_send.at[h],
-            recv_sem=map_recv.at[pair, source],
+            recv_sem=map_recv.at[pair // 2, source],
             device_id={seq_axis: owner_of(pair, i)},
             device_id_type=MESH,
         )
@@ -513,7 +513,7 @@
         return pltpu.make_async_remote_copy(
             src_ref=states.at[pair, target],
             dst_ref=s_ref.at[h],
-            send_sem=back_send.at[pair, target],
+            send_sem=back_send.at[pair // 2, target],
             recv_sem=back_recv.at[h],
             device_id={seq_axis: target},
             device_id_type=MESH,
@@ -756,23 +756,23 @@
     for t in range(count_pieces):
         near(t).wait()
         total[rows(t)] = total[rows(t)] + near_in[rows(t)].astype(F32)
+    for pair in range(pairs):
+        for i in range(2):
+
+            @pl.when((seq != owner_of(pair, i)) & (seq != peers - 1))
+            def _():
+                send_map(pair, i, seq).wait_send()
+
+            @pl.when(seq == owner_of(pair, i))
+            def _():
+                for k in range(1, peers):
+
+                    @pl.when(seq != k)
+                    def _():
+                        send_state(pair, i, k).wait_send()
     for t in range(count_pieces):
         cross(t).wait()
         y_ref[rows(t)] = (total[rows(t)] + cross_in[rows(t)].astype(F32)).astype(BF16)
-    for pair in range(pairs):
-        for i in range(2):
-
-            @pl.when((seq != owner_of(pair, i)) & (seq != peers - 1))
-            def _():
-                send_map(pair, i, seq).wait_send()
-
-            @pl.when(seq == owner_of(pair, i))
-            def _():
-                for k in range(1, peers):
-
-                    @pl.when(seq != k)
-                    def _():
-                        send_state(pair, i, k).wait_send()
 
 
 def fused(queries, keys, values, betas, gate, out_weight, seq_axis, axis):
@@ -832,8 +832,8 @@
             dma((heads,)),
             dma((4,)),
             dma((heads,)),
-            dma((pairs, peers)),
-            dma((pairs, peers)),
+            dma((pairs // 2, peers)),
+            dma((pairs // 2, peers)),
             dma((heads,)),
         ]
         + [dma((pieces,))] * 6,

time: 56.1 us -> 55.8 us (level)
  no operation moved by 1% of the time
where the time goes in v11:
time: 55.8 us; the launch traced here: 55.5 us
  Pallas kernels  54.5 us (98%)
  local copies, waits for them, and re-layouts  0.97 us (2%)
    pallas_call x1, Pallas kernels, fused(): pl.pallas_call(functools.partial(fused_kernel, seq_axis, peers, axis), in...  54.5 us

profile of v11, /device:TPU:24, one launch (start us, length us, event | category | flops | bytes accessed | tf_op | source)
XLA Modules:
  0.0 55.5 jit_solution(7872719997107621450)
XLA Ops:
  0.0 54.5 %shard_map.64 = bf16[512,1024]{1,0:T(8,128)(2,1)S(1)} custom-call(bf16[8,64,1024]{2,1,0:T(8,128)(2,1)} %bitcast.6, bf16[2,8,64,1024]{3,2,1,0:T(8,128)(2,1)} %bitcast.4, bf16[2,8,64,1024]{3,2,1,0:T(8,128)(2,1)} %bitcast.5, f32[8,2,512]{2,1,0:T(2,128)} %b_hbm.1, bf16[8,64,1024]{2,1,0:T(8,128)(2,1)} %bitcast.7, bf16[1024,4096]{1,0:T(8,128)(2,1)} %w_hbm.1), custom_call_target="tpu_custom_call" | custom-call | tf_op jit(solution)/shard_map/pallas_call | solution.py:795
  54.5 1.0 %copy.8 = bf16[512,1024]{1,0:T(8,128)(2,1)} copy(bf16[512,1024]{1,0:T(8,128)(2,1)S(1)} %shard_map.64) | data formatting | bytes 2097152
